TPU v7x, 16 devices: a whole 2x2x2 slice. The times are simulated.
16 devices in a mesh: dp: 2 (over z), fsdp: 8 (over y, x, core).
Axes of the slice: x: 2, y: 2, z: 2, core: 2. Of those that a mesh axis runs over, the one named last changes fastest.
Arguments:
- h_saved: bfloat16 [3, 16, 2048, 896], P(None, ('dp', 'fsdp'))
- grad_out: bfloat16 [16, 2048, 896], P(('dp', 'fsdp'))
- w_gate: bfloat16 [3, 896, 4864], P(None, 'fsdp')
- w_up: bfloat16 [3, 896, 4864], P(None, 'fsdp')
- w_down: bfloat16 [3, 4864, 896], P(None, 'fsdp')
Outputs:
- output 1: float32 [3, 896, 4864], P(None, 'fsdp')
- output 2: float32 [3, 896, 4864], P(None, 'fsdp')
- output 3: float32 [3, 4864, 896], P(None, 'fsdp')
- output 4: bfloat16 [16, 2048, 896], P(('dp', 'fsdp'))
All inputs are finite; a program needn't handle non-finite values.
Results may differ from a plain program's by a relative error of at most 0.00548976.
Values are sent between devices in bfloat16 or wider.
A program may use at most 1 GiB of HBM per device.

v0:
```python
import jax
import jax.numpy as jnp
from jax import lax
from jax.sharding import PartitionSpec as P

EPS = 1e-5


def layer_backward(h_in, g_acc, gate_w, up_w, down_w):
    x_full = h_in.astype(jnp.float32)
    inv_rms = lax.rsqrt(jnp.mean(x_full * x_full, axis=-1, keepdims=True) + EPS)
    norm_f = x_full * inv_rms
    norm_b = norm_f.astype(jnp.bfloat16)
    pre_gate = jnp.einsum("td,df->tf", norm_b, gate_w, preferred_element_type=jnp.float32)
    pre_up = jnp.einsum("td,df->tf", norm_b, up_w, preferred_element_type=jnp.float32)
    sig_gate = jax.nn.sigmoid(pre_gate)
    silu_gate = pre_gate * sig_gate
    act_b = (silu_gate * pre_up).astype(jnp.bfloat16)
    g_bf = g_acc.astype(jnp.bfloat16)
    d_act = jnp.einsum("td,fd->tf", g_bf, down_w, preferred_element_type=jnp.float32)
    grad_down = jnp.einsum("tf,td->fd", act_b, g_bf, preferred_element_type=jnp.float32)
    d_gate_b = (d_act * pre_up * sig_gate * (1.0 + pre_gate * (1.0 - sig_gate))).astype(jnp.bfloat16)
    d_up_b = (d_act * silu_gate).astype(jnp.bfloat16)
    grad_gate = jnp.einsum("td,tf->df", norm_b, d_gate_b, preferred_element_type=jnp.float32)
    grad_up = jnp.einsum("td,tf->df", norm_b, d_up_b, preferred_element_type=jnp.float32)
    d_norm = jnp.einsum("tf,df->td", d_gate_b, gate_w, preferred_element_type=jnp.float32) + jnp.einsum("tf,df->td", d_up_b, up_w, preferred_element_type=jnp.float32)
    d_x = inv_rms * (d_norm - norm_f * jnp.mean(d_norm * norm_f, axis=-1, keepdims=True))
    return g_acc + d_x, grad_gate, grad_up, grad_down


def reduce_grad(local_grad):
    shard_sum = lax.psum_scatter(local_grad, "fsdp", scatter_dimension=0, tiled=True)
    return lax.psum(shard_sum, "dp")


def solution(mesh):
    tok_spec = P(("dp", "fsdp"))
    stack_spec = P(None, ("dp", "fsdp"))
    weight_spec = P(None, "fsdp")

    def local_backward(h_saved, grad_out, gate_sh, up_sh, down_sh):
        n_layers = h_saved.shape[0]
        b_loc, seq_len, model_width = grad_out.shape
        tokens = b_loc * seq_len
        g_acc = grad_out.reshape(tokens, model_width).astype(jnp.float32)
        gate_parts = []
        up_parts = []
        down_parts = []
        for layer_idx in reversed(range(n_layers)):
            gate_w = lax.all_gather(gate_sh[layer_idx], "fsdp", axis=0, tiled=True)
            up_w = lax.all_gather(up_sh[layer_idx], "fsdp", axis=0, tiled=True)
            down_w = lax.all_gather(down_sh[layer_idx], "fsdp", axis=0, tiled=True)
            h_in = h_saved[layer_idx].reshape(tokens, model_width)
            g_acc, grad_gate, grad_up, grad_down = layer_backward(h_in, g_acc, gate_w, up_w, down_w)
            gate_parts.append(reduce_grad(grad_gate))
            up_parts.append(reduce_grad(grad_up))
            down_parts.append(reduce_grad(grad_down))
        d_h0 = g_acc.reshape(b_loc, seq_len, model_width).astype(jnp.bfloat16)
        return jnp.stack(gate_parts[::-1]), jnp.stack(up_parts[::-1]), jnp.stack(down_parts[::-1]), d_h0

    return jax.shard_map(local_backward, mesh=mesh, in_specs=(stack_spec, tok_spec, weight_spec, weight_spec, weight_spec), out_specs=(weight_spec, weight_spec, weight_spec, tok_spec), check_vma=False)
```

profile of v0, /device:TPU:0, one launch (start us, length us, event | category | flops | bytes accessed | tf_op | source)
XLA Modules:
  0.0 2001.9 jit_solution(12941573527681434915)
XLA Ops:
  7.2 3.8 fusion.104
  11.1 0.0 all-gather.21.cloned.1.call-start
  11.2 1.8 fusion.102
  13.0 3.7 fusion.103
  16.8 0.5 all-gather.29.cloned.1.call-update
  17.3 0.5 all-gather.27.cloned.1.call-update
  17.9 0.5 all-gather.25.cloned.1.call-update
  18.5 0.7 all-gather.35.cloned.1.call-update
  19.3 0.7 all-gather.33.cloned.1.call-update
  20.0 0.7 all-gather.31.cloned.1.call-update
  20.7 7.9 fusion.101
  28.6 6.0 copy.15
  34.7 2.8 fusion.55
  37.5 28.3 %all-gather.23.cloned.1.call-done = bf16[1,896,4864]{2,1,0:T(8,128)(2,1)} async-done(((bf16[1,112,4864]{2,1,0:T(8,128)(2,1)}), bf16[1,896,4864]{2,1,0:T(8,128)(2,1)}) %all-gather.23.cloned.1.call-update) | async-done | bytes 8716304 | tf_op jit(solution)/shard_map/all_gather | solution.py:50
  65.8 29.2 %fusion.37 = f32[2048,4864]{1,0:T(8,128)} fusion(bf16[1,896,4864]{2,1,0:T(8,128)(2,1)} %all-gather.23.cloned.1.call-done, bf16[1,1,2048,896]{2,3,1,0:T(8,128)(2,1)} %copy.15, f32[2048]{0:T(1024)S(1)} %add_rsqrt_fusion.1), kind=kOutput, calls=%fused_computation.55 | convolution fusion | flops 17856462848 | bytes 52240384 | tf_op jit(solution)/shard_map/td,df->tf/dot_general | solution.py:14
  94.9 24.4 %all-gather.21.cloned.1.call-done = bf16[1,896,4864]{2,1,0:T(8,128)(2,1)} async-done(((bf16[1,112,4864]{2,1,0:T(8,128)(2,1)}), bf16[1,896,4864]{2,1,0:T(8,128)(2,1)}) %all-gather.21.cloned.1.call-update) | async-done | bytes 8716304 | tf_op jit(solution)/shard_map/all_gather | solution.py:51
  119.4 29.2 %fusion.41 = f32[2048,4864]{1,0:T(8,128)} fusion(bf16[1,896,4864]{2,1,0:T(8,128)(2,1)} %all-gather.21.cloned.1.call-done, bf16[1,1,2048,896]{2,3,1,0:T(8,128)(2,1)} %copy.15, f32[2048]{0:T(1024)S(1)} %add_rsqrt_fusion.1), kind=kOutput, calls=%fused_computation.59 | convolution fusion | flops 17856462848 | bytes 52240384 | tf_op jit(solution)/shard_map/td,df->tf/dot_general | solution.py:15
  148.5 24.4 %all-gather.19.cloned.1.call-done = bf16[1,4864,896]{2,1,0:T(8,128)(2,1)} async-done(((bf16[1,608,896]{2,1,0:T(8,128)(2,1)}), bf16[1,4864,896]{2,1,0:T(8,128)(2,1)}) %all-gather.19.cloned.1.call-update) | async-done | bytes 8716304 | tf_op jit(solution)/shard_map/all_gather | solution.py:52
  172.9 62.6 %multiply_convert_fusion.7 = (bf16[2048,4864]{1,0:T(8,128)(2,1)}, bf16[2048,4864]{1,0:T(8,128)(2,1)}) fusion(f32[2048,4864]{1,0:T(8,128)} %fusion.37, f32[2048,4864]{1,0:T(8,128)} %fusion.41, bf16[1,4864,896]{2,1,0:T(8,128)(2,1)} %all-gather.19.cloned.1.call-done, bf16[1,2048,896]{2,1,0:T(8,128)(2,1)} %param.6), kind=kOutput, calls=%fused_computation.11 | convolution fusion | flops 17980456960 | bytes 131923968 | tf_op jit(solution)/shard_map/td,fd->tf/dot_general | solution.py:20
  235.5 25.2 %fusion.82 = f32[896,4864]{1,0:T(8,128)} fusion(bf16[2048,4864]{1,0:T(8,128)(2,1)} %get-tuple-element.21, bf16[1,1,2048,896]{2,3,1,0:T(8,128)(2,1)} %copy.15, f32[2048]{0:T(1024)S(1)} %add_rsqrt_fusion.1), kind=kOutput, calls=%fused_computation.90 | convolution fusion | flops 17856462848 | bytes 41033728 | tf_op jit(solution)/shard_map/td,tf->df/dot_general | solution.py:25
  260.8 25.2 %fusion.84 = f32[896,4864]{1,0:T(8,128)} fusion(bf16[2048,4864]{1,0:T(8,128)(2,1)} %get-tuple-element.22, bf16[1,1,2048,896]{2,3,1,0:T(8,128)(2,1)} %copy.15, f32[2048]{0:T(1024)S(1)} %add_rsqrt_fusion.1), kind=kOutput, calls=%fused_computation.91 | convolution fusion | flops 17856462848 | bytes 41033728 | tf_op jit(solution)/shard_map/td,tf->df/dot_general | solution.py:24
  286.0 0.0 reduce-scatter.26.cloned.1.call-start
  286.1 6.2 copy.10
  292.2 6.0 copy.16
  298.3 2.8 fusion.60
  301.1 0.6 add_rsqrt_fusion
  301.7 38.0 %fusion.5 = f32[4864,896]{1,0:T(8,128)} fusion(f32[2048,4864]{1,0:T(8,128)} %fusion.41, f32[2048,4864]{1,0:T(8,128)} %fusion.37, bf16[1,2048,896]{2,1,0:T(8,128)(2,1)} %param.6), kind=kOutput, calls=%fused_computation.17 | convolution fusion | flops 17910726656 | bytes 100794368 | tf_op jit(solution)/shard_map/tf,td->fd/dot_general | solution.py:21
  339.8 24.4 %fusion.35 = f32[2048,896]{0,1:T(8,128)S(1)} fusion(bf16[2048,4864]{1,0:T(8,128)(2,1)} %get-tuple-element.22, bf16[1,896,4864]{2,1,0:T(8,128)(2,1)} %all-gather.23.cloned.1.call-done), kind=kOutput, calls=%fused_computation.53 | convolution fusion | flops 17850957824 | bytes 35979264 | tf_op jit(solution)/shard_map/tf,df->td/dot_general | solution.py:26
  364.2 25.6 %fusion.51 = (f32[2048]{0:T(1024)S(1)}, f32[2048,896]{0,1:T(8,128)}) fusion(bf16[1,1,2048,896]{2,3,1,0:T(8,128)(2,1)S(1)} %copy-done.2, f32[2048]{0:T(1024)S(1)} %add_rsqrt_fusion.1, f32[2048,896]{0,1:T(8,128)S(1)} %fusion.35, bf16[2048,4864]{1,0:T(8,128)(2,1)} %get-tuple-element.21, bf16[1,896,4864]{2,1,0:T(8,128)(2,1)} %all-gather.21.cloned.1.call-done), kind=kOutput, calls=%fused_computation.69 | convolution fusion | flops 17860130816 | bytes 47005696 | tf_op jit(solution)/shard_map/tf,df->td/dot_general | solution.py:26
  389.7 8.2 fusion.54
  397.9 29.3 %fusion.27 = f32[2048,4864]{1,0:T(8,128)} fusion(bf16[1,896,4864]{2,1,0:T(8,128)(2,1)} %all-gather.29.cloned.1.call-done, bf16[1,1,2048,896]{2,3,1,0:T(8,128)(2,1)} %copy.16, f32[2048]{0:T(1024)S(1)} %copy-done.14), kind=kOutput, calls=%fused_computation.45 | convolution fusion | flops 17856462848 | bytes 52240384 | tf_op jit(solution)/shard_map/td,df->tf/dot_general | solution.py:14
  427.3 29.2 %fusion.31 = f32[2048,4864]{1,0:T(8,128)} fusion(bf16[1,896,4864]{2,1,0:T(8,128)(2,1)} %all-gather.27.cloned.1.call-done, bf16[1,1,2048,896]{2,3,1,0:T(8,128)(2,1)} %copy.16, f32[2048]{0:T(1024)S(1)} %copy-done.14), kind=kOutput, calls=%fused_computation.49 | convolution fusion | flops 17856462848 | bytes 52240384 | tf_op jit(solution)/shard_map/td,df->tf/dot_general | solution.py:15
  456.5 53.9 %multiply_convert_fusion.5 = (bf16[2048,4864]{1,0:T(8,128)(2,1)}, bf16[2048,4864]{1,0:T(8,128)(2,1)}) fusion(f32[2048,4864]{1,0:T(8,128)} %fusion.27, f32[2048,4864]{1,0:T(8,128)} %fusion.31, bf16[1,4864,896]{2,1,0:T(8,128)(2,1)} %all-gather.25.cloned.1.call-done, f32[2048,896]{0,1:T(8,128)} %fusion.54), kind=kOutput, calls=%fused_computation.7 | convolution fusion | flops 17982291968 | bytes 135593984 | tf_op jit(solution)/shard_map/td,fd->tf/dot_general | solution.py:20
  510.4 24.3 %fusion.88 = f32[896,4864]{1,0:T(8,128)} fusion(bf16[2048,4864]{1,0:T(8,128)(2,1)} %get-tuple-element.19, bf16[1,1,2048,896]{2,3,1,0:T(8,128)(2,1)S(1)} %copy-done.3, f32[2048]{0:T(1024)S(1)} %copy-done.14), kind=kOutput, calls=%fused_computation.92 | convolution fusion | flops 17856462848 | bytes 41033728 | tf_op jit(solution)/shard_map/td,tf->df/dot_general | solution.py:25
  534.7 25.2 %fusion.90 = f32[896,4864]{1,0:T(8,128)} fusion(bf16[2048,4864]{1,0:T(8,128)(2,1)} %get-tuple-element.20, bf16[1,1,2048,896]{2,3,1,0:T(8,128)(2,1)} %copy.16, f32[2048]{0:T(1024)S(1)} %copy-done.14), kind=kOutput, calls=%fused_computation.93 | convolution fusion | flops 17856462848 | bytes 41033728 | tf_op jit(solution)/shard_map/td,tf->df/dot_general | solution.py:24
  560.0 6.3 copy.14
  566.3 2.8 fusion.50
  569.1 0.6 add_rsqrt_fusion.2
  569.7 38.3 %fusion.4 = f32[4864,896]{1,0:T(8,128)} fusion(f32[2048,4864]{1,0:T(8,128)} %fusion.31, f32[2048,4864]{1,0:T(8,128)} %fusion.27, f32[2048,896]{0,1:T(8,128)} %fusion.54), kind=kOutput, calls=%fused_computation.16 | convolution fusion | flops 17912561664 | bytes 104464384 | tf_op jit(solution)/shard_map/tf,td->fd/dot_general | solution.py:21
  608.1 24.4 %fusion.25 = f32[2048,896]{0,1:T(8,128)S(1)} fusion(bf16[2048,4864]{1,0:T(8,128)(2,1)} %get-tuple-element.20, bf16[1,896,4864]{2,1,0:T(8,128)(2,1)} %all-gather.29.cloned.1.call-done), kind=kOutput, calls=%fused_computation.43 | convolution fusion | flops 17850957824 | bytes 35979264 | tf_op jit(solution)/shard_map/tf,df->td/dot_general | solution.py:26
  632.6 25.4 %fusion.56 = (f32[2048]{0:T(1024)S(1)}, f32[2048,896]{0,1:T(8,128)}) fusion(bf16[1,1,2048,896]{2,3,1,0:T(8,128)(2,1)S(1)} %copy-done.4, f32[2048]{0:T(1024)S(1)} %copy-done.14, f32[2048,896]{0,1:T(8,128)S(1)} %fusion.25, bf16[2048,4864]{1,0:T(8,128)(2,1)} %get-tuple-element.19, bf16[1,896,4864]{2,1,0:T(8,128)(2,1)} %all-gather.27.cloned.1.call-done), kind=kOutput, calls=%fused_computation.74 | convolution fusion | flops 17860130816 | bytes 47005696 | tf_op jit(solution)/shard_map/tf,df->td/dot_general | solution.py:26
  657.9 10.9 fusion.59
  668.8 29.3 %fusion.17 = f32[2048,4864]{1,0:T(8,128)} fusion(bf16[1,896,4864]{2,1,0:T(8,128)(2,1)} %all-gather.35.cloned.1.call-done, bf16[1,1,2048,896]{2,3,1,0:T(8,128)(2,1)} %copy.14, f32[2048]{0:T(1024)S(1)} %copy-done.13), kind=kOutput, calls=%fused_computation.35 | convolution fusion | flops 17856462848 | bytes 52240384 | tf_op jit(solution)/shard_map/td,df->tf/dot_general | solution.py:14
  698.2 29.2 %fusion.21 = f32[2048,4864]{1,0:T(8,128)} fusion(bf16[1,896,4864]{2,1,0:T(8,128)(2,1)} %all-gather.33.cloned.1.call-done, bf16[1,1,2048,896]{2,3,1,0:T(8,128)(2,1)} %copy.14, f32[2048]{0:T(1024)S(1)} %copy-done.13), kind=kOutput, calls=%fused_computation.39 | convolution fusion | flops 17856462848 | bytes 52240384 | tf_op jit(solution)/shard_map/td,df->tf/dot_general | solution.py:15
  727.3 54.1 %multiply_convert_fusion.3 = (bf16[2048,4864]{1,0:T(8,128)(2,1)}, bf16[2048,4864]{1,0:T(8,128)(2,1)}) fusion(f32[2048,4864]{1,0:T(8,128)} %fusion.17, f32[2048,4864]{1,0:T(8,128)} %fusion.21, bf16[1,4864,896]{2,1,0:T(8,128)(2,1)} %all-gather.31.cloned.1.call-done, f32[2048,896]{0,1:T(8,128)} %fusion.59), kind=kOutput, calls=%fused_computation.3 | convolution fusion | flops 17982291968 | bytes 135593984 | tf_op jit(solution)/shard_map/td,fd->tf/dot_general | solution.py:20
  781.5 24.0 %fusion.76 = f32[896,4864]{1,0:T(8,128)} fusion(bf16[2048,4864]{1,0:T(8,128)(2,1)} %get-tuple-element.17, bf16[1,1,2048,896]{2,3,1,0:T(8,128)(2,1)S(1)} %copy-done, f32[2048]{0:T(1024)S(1)} %copy-done.13), kind=kOutput, calls=%fused_computation.88 | convolution fusion | flops 17856462848 | bytes 41033728 | tf_op jit(solution)/shard_map/td,tf->df/dot_general | solution.py:25
  805.6 25.2 %fusion.78 = f32[896,4864]{1,0:T(8,128)} fusion(bf16[2048,4864]{1,0:T(8,128)(2,1)} %get-tuple-element.18, bf16[1,1,2048,896]{2,3,1,0:T(8,128)(2,1)} %copy.14, f32[2048]{0:T(1024)S(1)} %copy-done.13), kind=kOutput, calls=%fused_computation.89 | convolution fusion | flops 17856462848 | bytes 41033728 | tf_op jit(solution)/shard_map/td,tf->df/dot_general | solution.py:24
  830.8 38.6 %fusion.3 = f32[4864,896]{1,0:T(8,128)} fusion(f32[2048,4864]{1,0:T(8,128)} %fusion.21, f32[2048,4864]{1,0:T(8,128)} %fusion.17, f32[2048,896]{0,1:T(8,128)} %fusion.59), kind=kOutput, calls=%fused_computation.15 | convolution fusion | flops 17912561664 | bytes 104464384 | tf_op jit(solution)/shard_map/tf,td->fd/dot_general | solution.py:21
  869.5 90.3 %reduce-scatter.18.cloned.1.call-done = f32[112,4864]{1,0:T(8,128)} async-done(((f32[896,4864]{1,0:T(8,128)}), f32[112,4864]{1,0:T(8,128)}) %reduce-scatter.18.cloned.1.call-update) | async-done | bytes 2179088 | tf_op jit(solution)/shard_map/reduce_scatter | solution.py:32
  959.8 116.4 %reduce-scatter.12.cloned.1.call-done = f32[112,4864]{1,0:T(8,128)} async-done(((f32[896,4864]{1,0:T(8,128)}), f32[112,4864]{1,0:T(8,128)}) %reduce-scatter.12.cloned.1.call-update) | async-done | bytes 2179088 | tf_op jit(solution)/shard_map/reduce_scatter | solution.py:32
  1076.2 116.4 %reduce-scatter.24.cloned.1.call-done = f32[608,896]{1,0:T(8,128)} async-done(((f32[4864,896]{1,0:T(8,128)}), f32[608,896]{1,0:T(8,128)}) %reduce-scatter.24.cloned.1.call-update) | async-done | bytes 2179088 | tf_op jit(solution)/shard_map/reduce_scatter | solution.py:32
  1192.6 116.4 %reduce-scatter.16.cloned.1.call-done = f32[112,4864]{1,0:T(8,128)} async-done(((f32[896,4864]{1,0:T(8,128)}), f32[112,4864]{1,0:T(8,128)}) %reduce-scatter.16.cloned.1.call-update) | async-done | bytes 2179088 | tf_op jit(solution)/shard_map/reduce_scatter | solution.py:32
  1309.0 116.4 %reduce-scatter.10.cloned.1.call-done = f32[112,4864]{1,0:T(8,128)} async-done(((f32[896,4864]{1,0:T(8,128)}), f32[112,4864]{1,0:T(8,128)}) %reduce-scatter.10.cloned.1.call-update) | async-done | bytes 2179088 | tf_op jit(solution)/shard_map/reduce_scatter | solution.py:32
  1425.4 116.4 %reduce-scatter.22.cloned.1.call-done = f32[608,896]{1,0:T(8,128)} async-done(((f32[4864,896]{1,0:T(8,128)}), f32[608,896]{1,0:T(8,128)}) %reduce-scatter.22.cloned.1.call-update) | async-done | bytes 2179088 | tf_op jit(solution)/shard_map/reduce_scatter | solution.py:32
  1541.9 23.9 %fusion.15 = f32[2048,896]{0,1:T(8,128)S(1)} fusion(bf16[2048,4864]{1,0:T(8,128)(2,1)} %get-tuple-element.18, bf16[1,896,4864]{2,1,0:T(8,128)(2,1)} %all-gather.35.cloned.1.call-done), kind=kOutput, calls=%fused_computation.33 | convolution fusion | flops 17850957824 | bytes 35979264 | tf_op jit(solution)/shard_map/tf,df->td/dot_general | solution.py:26
  1565.8 25.4 %fusion.45 = (f32[2048]{0:T(1024)S(1)}, f32[2048,896]{0,1:T(8,128)}) fusion(bf16[1,1,2048,896]{2,3,1,0:T(8,128)(2,1)S(1)} %copy-done.1, f32[2048]{0:T(1024)S(1)} %copy-done.13, f32[2048,896]{0,1:T(8,128)S(1)} %fusion.15, bf16[2048,4864]{1,0:T(8,128)(2,1)} %get-tuple-element.17, bf16[1,896,4864]{2,1,0:T(8,128)(2,1)} %all-gather.33.cloned.1.call-done), kind=kOutput, calls=%fused_computation.63 | convolution fusion | flops 17860130816 | bytes 47005696 | tf_op jit(solution)/shard_map/tf,df->td/dot_general | solution.py:26
  1591.2 9.4 fusion.73
  1600.6 6.0 copy.13
  1606.6 373.9 %all-reduce.3.cloned.1.call-done = (f32[1,112,4864]{2,1,0:T(8,128)}, f32[1,112,4864]{2,1,0:T(8,128)}, f32[1,112,4864]{2,1,0:T(8,128)}, f32[1,112,4864]{2,1,0:T(8...) async-done(((f32[1,112,4864]{2,1,0:T(8,128)}, ...) | async-done | bytes 19611664 | tf_op jit(solution)/shard_map/psum | solution.py:33
  1980.5 6.8 pad_maximum_fusion.2
  1987.4 1.0 copy-done.10
  1988.4 0.6 copy-done.11
  1989.0 0.6 copy-done.12
  1989.6 5.3 pad_maximum_fusion
  (70 shorter events, 1.1 us)
Async XLA Ops:
  7.2 4.0 copy-start.6
  7.2 58.6 %all-gather.23.cloned.1.call-start = ((), (), s32[]{:S(2)}) async-start(), calls=%async_computation.20 | async-start | bytes 9805824 | tf_op jit(solution)/shard_map/all_gather | solution.py:50
  11.1 108.3 %all-gather.21.cloned.1.call-start = ((), (), s32[]{:S(2)}) async-start(), calls=%async_computation.19 | async-start | bytes 9805824 | tf_op jit(solution)/shard_map/all_gather | solution.py:51
  13.0 159.9 %all-gather.19.cloned.1.call-start = ((), (), s32[]{:S(2)}) async-start(), calls=%async_computation.18 | async-start | bytes 9805824 | tf_op jit(solution)/shard_map/all_gather | solution.py:52
  16.7 381.2 %all-gather.29.cloned.1.call-start = ((), (), s32[]{:S(2)}) async-start(), calls=%async_computation.23 | async-start | bytes 9805824 | tf_op jit(solution)/shard_map/all_gather | solution.py:50
  17.3 410.0 %all-gather.27.cloned.1.call-start = ((), (), s32[]{:S(2)}) async-start(), calls=%async_computation.22 | async-start | bytes 9805824 | tf_op jit(solution)/shard_map/all_gather | solution.py:51
  17.9 438.6 %all-gather.25.cloned.1.call-start = ((), (), s32[]{:S(2)}) async-start(), calls=%async_computation.21 | async-start | bytes 9805824 | tf_op jit(solution)/shard_map/all_gather | solution.py:52
  18.5 650.4 %all-gather.35.cloned.1.call-start = ((), (), s32[]{:S(2)}) async-start(), calls=%async_computation.26 | async-start | bytes 9805824 | tf_op jit(solution)/shard_map/all_gather | solution.py:50
  19.2 678.9 %all-gather.33.cloned.1.call-start = ((), (), s32[]{:S(2)}) async-start(), calls=%async_computation.25 | async-start | bytes 9805824 | tf_op jit(solution)/shard_map/all_gather | solution.py:51
  20.0 707.4 %all-gather.31.cloned.1.call-start = ((), (), s32[]{:S(2)}) async-start(), calls=%async_computation.24 | async-start | bytes 9805824 | tf_op jit(solution)/shard_map/all_gather | solution.py:52
  20.7 848.8 %reduce-scatter.20.cloned.1.call-start = ((), (), s32[]{:S(2)}) async-start(), calls=%async_computation.14 | async-start | bytes 19611648 | tf_op jit(solution)/shard_map/reduce_scatter | solution.py:32
  260.8 608.8 %reduce-scatter.14.cloned.1.call-start = ((), (), s32[]{:S(2)}) async-start(), calls=%async_computation.11 | async-start | bytes 19611648 | tf_op jit(solution)/shard_map/reduce_scatter | solution.py:32
  286.0 583.5 %reduce-scatter.26.cloned.1.call-start = ((), (), s32[]{:S(2)}) async-start(), calls=%async_computation.17 | async-start | bytes 19611648 | tf_op jit(solution)/shard_map/reduce_scatter | solution.py:32
  339.7 620.1 %reduce-scatter.18.cloned.1.call-start = ((), (), s32[]{:S(2)}) async-start(), calls=%async_computation.13 | async-start | bytes 19611648 | tf_op jit(solution)/shard_map/reduce_scatter | solution.py:32
  339.8 24.4 %copy-start.2 = (bf16[1,1,2048,896]{2,3,1,0:T(8,128)(2,1)S(1)}, bf16[1,1,2048,896]{2,3,1,0:T(8,128)(2,1)}, u32[]{:S(2)}) copy-start(bf16[1,1,2048,896]{2,3,1,0:T(8,128)(2,1)} %copy.15) | copy-start | bytes 11010052
  364.1 25.6 %copy-start.5 = (bf16[1,2048,896]{1,2,0:T(8,128)(2,1)S(1)}, bf16[1,2048,896]{1,2,0:T(8,128)(2,1)}, u32[]{:S(2)}) copy-start(bf16[1,2048,896]{1,2,0:T(8,128)(2,1)} %copy.10) | copy-start | bytes 11010052
  389.7 8.2 copy-start.14
  456.5 53.9 %copy-start.3 = (bf16[1,1,2048,896]{2,3,1,0:T(8,128)(2,1)S(1)}, bf16[1,1,2048,896]{2,3,1,0:T(8,128)(2,1)}, u32[]{:S(2)}) copy-start(bf16[1,1,2048,896]{2,3,1,0:T(8,128)(2,1)} %copy.16) | copy-start | bytes 11010052
  534.7 541.5 %reduce-scatter.12.cloned.1.call-start = ((), (), s32[]{:S(2)}) async-start(), calls=%async_computation.10 | async-start | bytes 19611648 | tf_op jit(solution)/shard_map/reduce_scatter | solution.py:32
  559.9 632.7 %reduce-scatter.24.cloned.1.call-start = ((), (), s32[]{:S(2)}) async-start(), calls=%async_computation.16 | async-start | bytes 19611648 | tf_op jit(solution)/shard_map/reduce_scatter | solution.py:32
  608.1 701.0 %reduce-scatter.16.cloned.1.call-start = ((), (), s32[]{:S(2)}) async-start(), calls=%async_computation.12 | async-start | bytes 19611648 | tf_op jit(solution)/shard_map/reduce_scatter | solution.py:32
  608.1 24.5 %copy-start.4 = (bf16[1,1,2048,896]{2,3,1,0:T(8,128)(2,1)S(1)}, bf16[1,1,2048,896]{2,3,1,0:T(8,128)(2,1)}, u32[]{:S(2)}) copy-start(bf16[1,1,2048,896]{2,3,1,0:T(8,128)(2,1)} %copy.16) | copy-start | bytes 11010052
  657.9 10.9 copy-start.13
  727.3 54.1 %copy-start = (bf16[1,1,2048,896]{2,3,1,0:T(8,128)(2,1)S(1)}, bf16[1,1,2048,896]{2,3,1,0:T(8,128)(2,1)}, u32[]{:S(2)}) copy-start(bf16[1,1,2048,896]{2,3,1,0:T(8,128)(2,1)} %copy.14) | copy-start | bytes 11010052
  805.5 619.9 %reduce-scatter.10.cloned.1.call-start = ((), (), s32[]{:S(2)}) async-start(), calls=%async_computation.9 | async-start | bytes 19611648 | tf_op jit(solution)/shard_map/reduce_scatter | solution.py:32
  830.8 711.1 %reduce-scatter.22.cloned.1.call-start = ((), (), s32[]{:S(2)}) async-start(), calls=%async_computation.15 | async-start | bytes 19611648 | tf_op jit(solution)/shard_map/reduce_scatter | solution.py:32
  869.4 1111.1 %all-reduce.3.cloned.1.call-start = ((), (), s32[]{:S(2)}) async-start(), calls=%async_computation.27 | async-start | bytes 39223296 | tf_op jit(solution)/shard_map/psum | solution.py:33
  1541.9 23.9 %copy-start.1 = (bf16[1,1,2048,896]{2,3,1,0:T(8,128)(2,1)S(1)}, bf16[1,1,2048,896]{2,3,1,0:T(8,128)(2,1)}, u32[]{:S(2)}) copy-start(bf16[1,1,2048,896]{2,3,1,0:T(8,128)(2,1)} %copy.14) | copy-start | bytes 11010052
  1980.5 6.8 copy-start.7
  1980.5 6.8 copy-start.8
  1980.5 6.8 copy-start.9
  1980.5 7.8 copy-start.10
  1980.5 8.5 copy-start.11
  1980.5 9.1 copy-start.12
Sparse Core Ops, SparseCore 0:
  11.2 54.5 all-gather.22
  67.6 51.6 all-gather.20
  121.2 51.6 all-gather.18
  174.6 51.6 all-gather.28
  228.0 51.6 all-gather.26
  281.5 51.6 all-gather.24
  335.0 51.6 all-gather.34
  388.6 51.6 all-gather.32
  442.2 51.6 all-gather.30
  497.4 112.8 reduce-scatter.19
  613.9 112.8 reduce-scatter.13
  730.4 112.8 reduce-scatter.25
  846.9 112.8 reduce-scatter.17
  963.3 112.8 reduce-scatter.11
  1079.7 112.8 reduce-scatter.23
  1196.1 112.8 reduce-scatter.15
  1312.5 112.8 reduce-scatter.9
  1428.9 112.8 reduce-scatter.21
  1545.4 435.0 all-reduce.2
where the time goes:
time: 2010 us; the launch traced here: 2000 us
  waiting for transfers between devices  1130 us (56%)
  matrix products  759 us (38%)
  other arithmetic  50.2 us (2%)
  local copies, waits for them, and re-layouts  50.1 us (2%)
    reduce_scatter x9, waiting for transfers between devices, reduce_grad(): lax.psum_scatter(local_grad, 'fsdp', scatter_dimension=0, tiled=True)  672 us
    psum x1, waiting for transfers between devices, reduce_grad(): return lax.psum(shard_sum, 'dp')  374 us
    dot_general x3, matrix products, layer_backward(): jnp.einsum('td,fd->tf', g_bf, down_w, preferred_element_type=jnp.float32)  171 us
    dot_general x3, matrix products, layer_backward(): jnp.einsum('tf,td->fd', act_b, g_bf, preferred_element_type=jnp.float32)  115 us
    dot_general x3, matrix products, layer_backward(): jnp.einsum('td,df->tf', norm_b, gate_w, preferred_element_type=jnp.float32)  87.8 us
    dot_general x3, matrix products, layer_backward(): jnp.einsum('td,df->tf', norm_b, up_w, preferred_element_type=jnp.float32)  87.6 us
    dot_general x3, matrix products, layer_backward(): jnp.einsum('tf,df->td', d_up_b, up_w, preferred_element_type=jnp.float32)  76.3 us
    dot_general x3, matrix products, layer_backward(): jnp.einsum('td,tf->df', norm_b, d_gate_b, preferred_element_type=jnp.floa...  75.5 us
  transfers between devices with their start and end apart: 19, of which 10 were waited for; matrix products, arithmetic and copies ran while one was open for 42% of the time, Pallas kernels for 0%

commit v1 on v0

v1 whole, which is shorter than its diff:
```python
import jax
import jax.numpy as jnp
from jax import lax
from jax.experimental import pallas as pl
from jax.experimental.pallas import tpu as pltpu
from jax.sharding import PartitionSpec as P

EPS = 1e-5
MESH = pl.DeviceIdType.MESH
F32, BF16 = jnp.float32, jnp.bfloat16
L, T, D, FF = 3, 2048, 896, 4864
NJ, FC = 19, 256
NI = 10
NT = L * NI
TB = 512
UB = 256
R1, R2, R3 = 3, 3, 3
PF = 5
ND = 3
WS = 8
ORDER = (0, 4, 2, 6, 1, 3, 5, 7)


def dg(a, b, ca, cb):
    return lax.dot_general(a, b, (((ca,), (cb,)), ((), ())), preferred_element_type=F32)


def kernel(h, gout, wgu, wd, og, ou, od, dh0, wbg, wbd, dnx, gbuf,
           n_v, gb_v, dn_v, wg_v, wd_v, Gg, Gu, Gd, r1g, r1u, r1d, r2g, r2u, r2d, r3g, r3u, r3d,
           st_h, st_n, st_dnx, st_g,
           w_recv, w_send, rl_send, load_sem, s1_send, s1_recv, s2_send, s2_recv, s3_send, s3_recv,
           o_send, o_recv, x_send, x_recv, st_sem, cr1, cr2, cr3):
    z, f = lax.axis_index("dp"), lax.axis_index("fsdp")
    y, x, c = f // 4, (f // 2) % 2, f % 2

    def dev(zz, yy, xx, cc):
        return (zz, 4 * yy + 2 * xx + cc)

    xn, yn, zn = dev(z, y, 1 - x, c), dev(z, 1 - y, x, c), dev(1 - z, y, x, c)
    sib = dev(z, y, x, 1 - c)

    def rcopy(src, dst, ss, rs, to):
        return pltpu.make_async_remote_copy(src, dst, ss, rs, device_id=to, device_id_type=MESH)

    def wait_bytes(ref, sem):
        pltpu.make_async_copy(ref, ref, sem).wait()

    bar = pltpu.get_barrier_semaphore()
    for k in range(1, 16):
        g = (8 * z + f + k) % 16
        pl.semaphore_signal(bar, inc=1, device_id=(g // 8, g % 8), device_id_type=MESH)
    pl.semaphore_wait(bar, 15)

    def layer_of(t):
        return L - 1 - t // NI

    def drow(yy, xx, cc):
        return pl.multiple_of(jnp.where(cc == 0, 32 * (2 * xx + yy), 128 + 32 * (2 * yy + xx)), 32)

    def grow(yy, xx, n=224):
        return pl.ds(pl.multiple_of(224 * (2 * yy + xx), 16), n)

    def has(t, cc):
        return 2 * (t % NI) + cc < NJ

    def w_sends(t, cc):
        l, i = layer_of(t), t % NI
        j = 2 * i + cc
        sg, sd = wgu.at[l, j], wd.at[l, j]
        dgu = wbg.at[l, i, pl.ds(pl.multiple_of(112 * f, 16), 112)]
        dd = wbd.at[l, i, pl.ds(drow(y, x, c), 32)]
        direct = t < ND
        prim = jnp.logical_or(direct, t % 2 == z)
        slot = t % WS
        out = []
        for k, (to, cond) in enumerate((
            (dev(z, y, x, cc), cc != c),
            (dev(z, y, 1 - x, cc), prim),
            (dev(z, 1 - y, x, cc), prim),
            (dev(z, 1 - y, 1 - x, cc), direct),
        )):
            out.append((cond, [
                rcopy(sg, dgu, w_send.at[slot, cc, k, 0], w_recv.at[t, 2 * k], to),
                rcopy(sd, dd, w_send.at[slot, cc, k, 1], w_recv.at[t, 2 * k + 1], to),
            ]))
        return out

    def each_send(t, act):
        for cc in range(2):
            @pl.when(has(t, cc))
            def _():
                for cond, cps in w_sends(t, cc):
                    @pl.when(cond)
                    def _():
                        for cp in cps:
                            act(cp)

    def w_issue(t):
        each_send(t, lambda cp: cp.start())

    def w_drain(t):
        each_send(t, lambda cp: cp.wait_send())

    def relay(t, yy, xx, k, to, base):
        l, i = layer_of(t), t % NI
        g = wbg.at[l, i, grow(yy, xx)]
        cps = [rcopy(g, g, rl_send.at[t % 4, base], w_recv.at[t, 2 * k], to)]
        for cc in range(2):
            d = wbd.at[l, i, pl.ds(drow(yy, xx, cc), 32)]
            cps.append(rcopy(d, d, rl_send.at[t % 4, base + 1 + cc], w_recv.at[t, 2 * k + 1], to))
        return cps

    def relays1(t):
        return relay(t, y, 1 - x, 1, zn, 0) + relay(t, 1 - y, x, 2, zn, 3)

    def relays2(t):
        return relay(t, 1 - y, 1 - x, 3, zn, 9)

    def wait_kind(t, k):
        l, i = layer_of(t), t % NI
        wait_bytes(wbg.at[l, i, pl.ds(0, 224)], w_recv.at[t, 2 * k])
        wait_bytes(wbd.at[l, i, pl.ds(0, 64)], w_recv.at[t, 2 * k + 1])

    def relayed(t):
        return jnp.logical_and(t >= ND, jnp.logical_and(t < NT, has(t, c)))

    def w_relay1(t):
        @pl.when(jnp.logical_and(relayed(t), t % 2 == z))
        def _():
            wait_kind(t, 1)
            wait_kind(t, 2)
            for cp in relays1(t):
                cp.start()
            @pl.when((t // 2) % 2 == 0)
            def _():
                for cp in relay(t, y, 1 - x, 3, yn, 6):
                    cp.start()
            @pl.when((t // 2) % 2 == 1)
            def _():
                for cp in relay(t, 1 - y, x, 3, xn, 6):
                    cp.start()

    def w_relay2(t):
        @pl.when(jnp.logical_and(relayed(t), t % 2 == z))
        def _():
            wait_kind(t, 3)
            for cp in relays2(t):
                cp.start()

    def w_relay_drain(t):
        @pl.when(jnp.logical_and(relayed(t), t % 2 == z))
        def _():
            for cp in relays1(t) + relay(t, y, 1 - x, 3, yn, 6) + relays2(t):
                cp.wait_send()

    def loads(t):
        l, i = layer_of(t), t % NI
        s = t % 2
        j = 2 * i + c
        cps = []
        for q in range(4):
            qq = (q + 2 * y + x) % 4
            yy, xx = qq // 2, qq % 2
            if q == 0:
                for mine in (True, False):
                    ff = f if mine else 4 * y + 2 * x + 1 - c
                    cc = c if mine else 1 - c
                    rg, rd = pl.ds(pl.multiple_of(112 * ff, 16), 112), pl.ds(drow(y, x, cc), 32)
                    cps.append((wgu.at[l, j] if mine else wbg.at[l, i, rg], wg_v.at[s, rg]))
                    cps.append((wd.at[l, j] if mine else wbd.at[l, i, rd], wd_v.at[s, rd]))
            else:
                rg = grow(yy, xx)
                cps.append((wbg.at[l, i, rg], wg_v.at[s, rg]))
                for cc in range(2):
                    rd = pl.ds(drow(yy, xx, cc), 32)
                    cps.append((wbd.at[l, i, rd], wd_v.at[s, rd]))
        return cps

    def w_load(t):
        @pl.when(jnp.logical_and(t < NT, has(t, c)))
        def _():
            l, i = layer_of(t), t % NI
            wait_bytes(wbg.at[l, i, pl.ds(0, 112)], w_recv.at[t, 0])
            wait_bytes(wbd.at[l, i, pl.ds(0, 32)], w_recv.at[t, 1])
            @pl.when(jnp.logical_or(t < ND, t % 2 != z))
            def _():
                for k in (1, 2, 3):
                    wait_kind(t, k)
            for src, dst in loads(t):
                pltpu.make_async_copy(src, dst, load_sem.at[0 if src.shape[-1] == 512 else 1]).start()

    def w_load_wait(t):
        wait_bytes(wg_v.at[t % 2], load_sem.at[0])
        wait_bytes(wd_v.at[t % 2], load_sem.at[1])

    for t in range(PF):
        w_issue(jnp.int32(t))

    own0 = T * c
    oth0 = T * (1 - c)

    def rows(base, b):
        return pl.ds(pl.multiple_of(base + b * UB, UB), UB)

    def norm_block(xf):
        r = lax.rsqrt(jnp.mean(xf * xf, axis=-1, keepdims=True) + EPS)
        return r, xf * r

    gl = pltpu.make_async_copy(gout, gb_v.at[pl.ds(pl.multiple_of(own0, T), T)], st_sem.at[0])
    gr = rcopy(gout, gb_v.at[pl.ds(pl.multiple_of(own0, T), T)], x_send.at[0], x_recv.at[0], sib)
    gl.start()
    gr.start()

    NB = T // UB

    def first_blocks(b, _):
        s = b % 2
        cp = pltpu.make_async_copy(h.at[L - 1, pl.ds(pl.multiple_of(b * UB, UB), UB)], st_n.at[s], st_sem.at[3])
        cp.start()
        cp.wait()
        _, nf = norm_block(st_n[s].astype(F32))
        n_v[rows(own0, b), :] = nf.astype(BF16)
        rcopy(n_v.at[rows(own0, b)], n_v.at[rows(own0, b)], x_send.at[1], x_recv.at[1], sib).start()
        return 0

    lax.fori_loop(0, NB, first_blocks, 0)

    def half(base):
        return pl.ds(pl.multiple_of(base, T), T)

    def exchange_done():
        wait_bytes(n_v.at[half(oth0)], x_recv.at[1])
        wait_bytes(gb_v.at[half(oth0)], x_recv.at[0])
        wait_bytes(n_v.at[half(own0)], x_send.at[1])
        wait_bytes(gb_v.at[half(own0)], x_send.at[0])

    gl.wait()
    w_load(jnp.int32(0))
    exchange_done()

    def compute(s, n):
        i = s % NI
        ws, gs = s % 2, n % 2
        w_load_wait(s)
        wg, wdd = wg_v.at[ws], wd_v.at[ws]

        def block(b, _):
            rw = pl.ds(pl.multiple_of(b * TB, TB), TB)
            nb, gbb = n_v[rw, :], gb_v[rw, :]
            uv = dg(nb, wg[...], 1, 0)
            u, v = uv[:, :FC], uv[:, FC:]
            da = dg(gbb, wdd[...], 1, 1)
            sg = jax.nn.sigmoid(u)
            sl = u * sg
            a = (sl * v).astype(BF16)
            du = (da * v * sg * (1.0 + u * (1.0 - sg))).astype(BF16)
            dv = (da * sl).astype(BF16)
            duv = jnp.concatenate([du, dv], axis=1)
            dnb = dg(duv, wg[...], 1, 1)

            @pl.when(i == 0)
            def _():
                dn_v[rw, :] = dnb

            @pl.when(i > 0)
            def _():
                dn_v[rw, :] += dnb

            g2 = dg(nb, duv, 0, 0)
            g3 = dg(a, gbb, 0, 0).reshape(8, 32, D)

            def put(add):
                for q in range(4):
                    yy, xx = q // 2, q % 2
                    pg, pu = g2[224 * q:224 * q + 224, :FC], g2[224 * q:224 * q + 224, FC:]
                    if add:
                        Gg[gs, 2 * xx + yy] += pg
                        Gu[gs, q] += pu
                    else:
                        Gg[gs, 2 * xx + yy] = pg
                        Gu[gs, q] = pu
                if add:
                    Gd[gs] += g3
                else:
                    Gd[gs] = g3

            @pl.when(b == 0)
            def _():
                put(False)

            @pl.when(b > 0)
            def _():
                put(True)

            return 0

        lax.fori_loop(0, 2 * T // TB, block, 0)

    def num(s):
        return s - c * (s // NI)

    def valid(s):
        return jnp.logical_and(jnp.logical_and(s >= 0, s < NT), 2 * (s % NI) + c < NJ)

    def s1(n):
        gs, rs, k = n % 2, n % R1, n % 2
        return [
            rcopy(Gg.at[gs, pl.ds(2 * (1 - x), 2)], r1g.at[rs], s1_send.at[k, 0], s1_recv.at[rs, 0], xn),
            rcopy(Gd.at[gs, pl.ds(2 * (1 - x), 2)], r1d.at[rs, pl.ds(0, 2)], s1_send.at[k, 1], s1_recv.at[rs, 1], xn),
            rcopy(Gu.at[gs, pl.ds(2 * (1 - y), 2)], r1u.at[rs], s1_send.at[k, 2], s1_recv.at[rs, 2], yn),
            rcopy(Gd.at[gs, pl.ds(4 + 2 * (1 - y), 2)], r1d.at[rs, pl.ds(2, 2)], s1_send.at[k, 3], s1_recv.at[rs, 3], yn),
        ]

    def s2(n):
        rs, qs, k = n % R1, n % R2, n % 2
        return [
            rcopy(r1g.at[rs, 1 - y], r2g.at[qs], s2_send.at[k, 0], s2_recv.at[qs, 0], yn),
            rcopy(r1d.at[rs, 1 - y], r2d.at[qs, 0], s2_send.at[k, 1], s2_recv.at[qs, 1], yn),
            rcopy(r1u.at[rs, 1 - x], r2u.at[qs], s2_send.at[k, 2], s2_recv.at[qs, 2], xn),
            rcopy(r1d.at[rs, 3 - x], r2d.at[qs, 1], s2_send.at[k, 3], s2_recv.at[qs, 3], xn),
        ]

    def s3(n):
        qs, ps, k = n % R2, n % R3, n % 2
        return [
            rcopy(r2g.at[qs], r3g.at[ps], s3_send.at[k, 0], s3_recv.at[ps, 0], zn),
            rcopy(r2u.at[qs], r3u.at[ps], s3_send.at[k, 1], s3_recv.at[ps, 1], zn),
            rcopy(r2d.at[qs], r3d.at[ps], s3_send.at[k, 2], s3_recv.at[ps, 2], zn),
        ]

    def outs(s, n):
        l, j = layer_of(s), 2 * (s % NI) + c
        ps, k = n % R3, n % 2
        mine, other = pl.ds(pl.multiple_of(112 * c, 8), 112), pl.ds(pl.multiple_of(112 * (1 - c), 8), 112)
        local = [
            pltpu.make_async_copy(r3g.at[ps, mine], og.at[l, j], o_send.at[k, 0]),
            pltpu.make_async_copy(r3u.at[ps, mine], ou.at[l, j], o_send.at[k, 1]),
            pltpu.make_async_copy(r3d.at[ps, c], od.at[l, j], o_send.at[k, 2]),
        ]
        remote = [
            rcopy(r3g.at[ps, other], og.at[l, j], o_send.at[k, 3], o_recv.at[0], sib),
            rcopy(r3u.at[ps, other], ou.at[l, j], o_send.at[k, 4], o_recv.at[1], sib),
            rcopy(r3d.at[ps, 1 - c], od.at[l, j], o_send.at[k, 5], o_recv.at[2], sib),
        ]
        return local + remote

    def credit(sem, to):
        pl.semaphore_signal(sem, inc=1, device_id=to, device_id_type=MESH)

    def stage1(s):
        @pl.when(valid(s))
        def _():
            n = num(s)
            @pl.when(n >= R1)
            def _():
                pl.semaphore_wait(cr1.at[0], 1)
                pl.semaphore_wait(cr1.at[1], 1)
            for cp in s1(n):
                cp.start()

    last = NT - L * c

    def stage2(s):
        @pl.when(valid(s))
        def _():
            n = num(s)
            gs, rs = n % 2, n % R1
            for cp in s1(n):
                cp.wait_recv()
            r1g[rs] += Gg[gs, pl.ds(2 * x, 2)]
            r1u[rs] += Gu[gs, pl.ds(2 * y, 2)]
            r1d[rs, 0:2] += Gd[gs, pl.ds(2 * x, 2)]
            r1d[rs, 2:4] += Gd[gs, pl.ds(4 + 2 * y, 2)]
            @pl.when(n >= R2)
            def _():
                pl.semaphore_wait(cr2.at[0], 1)
                pl.semaphore_wait(cr2.at[1], 1)
            for cp in s2(n):
                cp.start()

    def stage3(s):
        @pl.when(valid(s))
        def _():
            n = num(s)
            rs, qs = n % R1, n % R2
            for cp in s2(n):
                cp.wait_recv()
            r2g[qs] += r1g[rs, y]
            r2u[qs] += r1u[rs, x]
            r2d[qs, 0] += r1d[rs, y]
            r2d[qs, 1] += r1d[rs, 2 + x]
            @pl.when(n >= R3)
            def _():
                pl.semaphore_wait(cr3, 1)
            for cp in s3(n):
                cp.start()
            for cp in s2(n):
                cp.wait_send()
            @pl.when(n + R1 < last)
            def _():
                credit(cr1.at[0], xn)
                credit(cr1.at[1], yn)

    def stage4(s):
        @pl.when(valid(s))
        def _():
            n = num(s)
            qs, ps = n % R2, n % R3
            for cp in s3(n):
                cp.wait_recv()
            r3g[ps] += r2g[qs]
            r3u[ps] += r2u[qs]
            r3d[ps] += r2d[qs]
            for cp in outs(s, n):
                cp.start()
            for cp in s3(n):
                cp.wait_send()
            @pl.when(n + R2 < last)
            def _():
                credit(cr2.at[0], yn)
                credit(cr2.at[1], xn)

    def stage5(s):
        @pl.when(valid(s))
        def _():
            n = num(s)
            cps = outs(s, n)
            for cp in cps[:3]:
                cp.wait()
            for cp in cps[3:]:
                cp.wait_send()
            @pl.when(n + R3 < last)
            def _():
                credit(cr3, zn)

    def free_g(s):
        @pl.when(valid(s))
        def _():
            for cp in s1(num(s)):
                cp.wait_send()

    def dn_copy(b):
        return rcopy(dn_v.at[rows(oth0, b)], dnx.at[pl.ds(b * UB, UB)], x_send.at[2], x_recv.at[2 + b], sib)

    def dn_send():
        for b in range(NB):
            dn_copy(b).start()

    def boundary(s):
        l = layer_of(s)

        def fetch(b):
            r = pl.ds(pl.multiple_of(b * UB, UB), UB)
            pltpu.make_async_copy(h.at[l, r], st_h, st_sem.at[1]).start()
            @pl.when(l > 0)
            def _():
                pltpu.make_async_copy(h.at[jnp.maximum(l - 1, 0), r], st_n.at[0], st_sem.at[3]).start()
            @pl.when(l < L - 1)
            def _():
                pltpu.make_async_copy(gbuf.at[r], st_g, st_sem.at[2]).start()

        def block(b, _):
            r = pl.ds(pl.multiple_of(b * UB, UB), UB)
            ro = rows(own0, b)
            fetch(b)
            wait_bytes(dnx.at[r], x_recv.at[2 + b])
            pltpu.make_async_copy(dnx.at[r], st_dnx, st_sem.at[4]).start()
            wait_bytes(st_h, st_sem.at[1])
            @pl.when(l < L - 1)
            def _():
                wait_bytes(st_g, st_sem.at[2])
            @pl.when(l == L - 1)
            def _():
                st_g[...] = gb_v[ro, :].astype(F32)
            wait_bytes(st_dnx, st_sem.at[4])
            rr, nf = norm_block(st_h[...].astype(F32))
            dn = dn_v[ro, :] + st_dnx[...]
            m = jnp.mean(dn * nf, axis=-1, keepdims=True)
            g = st_g[...] + rr * (dn - nf * m)
            gb_v[ro, :] = g.astype(BF16)

            @pl.when(l > 0)
            def _():
                st_g[...] = g
                cg = pltpu.make_async_copy(st_g, gbuf.at[r], st_sem.at[5])
                cg.start()
                rcopy(gb_v.at[ro], gb_v.at[ro], x_send.at[0], x_recv.at[0], sib).start()
                wait_bytes(st_n.at[0], st_sem.at[3])
                _, nf2 = norm_block(st_n[0].astype(F32))
                n_v[ro, :] = nf2.astype(BF16)
                rcopy(n_v.at[ro], n_v.at[ro], x_send.at[1], x_recv.at[1], sib).start()
                cg.wait()

            @pl.when(l == 0)
            def _():
                pltpu.make_async_copy(gb_v.at[ro], dh0.at[r], st_sem.at[6]).start()
            return 0

        lax.fori_loop(0, NB, block, 0)
        wait_bytes(dn_v.at[half(oth0)], x_send.at[2])

        @pl.when(l > 0)
        def _():
            exchange_done()

        @pl.when(l == 0)
        def _():
            wait_bytes(dh0, st_sem.at[6])

    def step(s, _):
        edge = jnp.logical_and(s % NI == NI - 1, s < NT)

        @pl.when(valid(s))
        def _():
            compute(s, num(s))

        stage1(s)

        @pl.when(edge)
        def _():
            dn_send()

        @pl.when(s + PF < NT)
        def _():
            @pl.when(s + PF >= WS)
            def _():
                w_drain(s + PF - WS)
            w_issue(s + PF)

        w_relay1(s + 3)
        stage2(s - 1)
        w_relay2(s + 2)
        stage3(s - 2)
        w_load(s + 1)
        stage4(s - 3)
        stage5(s - 4)
        free_g(s - 1)
        w_relay_drain(s + 1)

        @pl.when(edge)
        def _():
            boundary(s)
        return 0

    lax.fori_loop(0, NT + 4, step, 0)
    for t in range(NT - WS, NT):
        w_drain(jnp.int32(t))

    def out_done(cnt):
        wait_bytes(og.at[:, pl.ds(0, cnt)], o_recv.at[0])
        wait_bytes(ou.at[:, pl.ds(0, cnt)], o_recv.at[1])
        wait_bytes(od.at[:, pl.ds(0, cnt)], o_recv.at[2])

    @pl.when(c == 0)
    def _():
        out_done(9)

    @pl.when(c == 1)
    def _():
        out_done(10)


def call(h, gout, wgu, wd):
    A = pl.BlockSpec(memory_space=pl.ANY)
    V, S = pltpu.VMEM, pltpu.SemaphoreType
    sd = jax.ShapeDtypeStruct
    return pl.pallas_call(
        kernel,
        out_shape=(
            sd((L, NJ, 112, FC), F32), sd((L, NJ, 112, FC), F32), sd((L, NJ, 32, D), F32), sd((T, D), BF16),
            sd((L, NI, D, 2 * FC), BF16), sd((L, NI, FC, D), BF16), sd((T, D), F32), sd((T, D), F32),
        ),
        in_specs=[A] * 4,
        out_specs=(A,) * 8,
        scratch_shapes=[
            V((2 * T, D), BF16), V((2 * T, D), BF16), V((2 * T, D), F32),
            V((2, D, 2 * FC), BF16), V((2, FC, D), BF16),
            V((2, 4, 224, FC), F32), V((2, 4, 224, FC), F32), V((2, 8, 32, D), F32),
            V((R1, 2, 224, FC), F32), V((R1, 2, 224, FC), F32), V((R1, 4, 32, D), F32),
            V((R2, 224, FC), F32), V((R2, 224, FC), F32), V((R2, 2, 32, D), F32),
            V((R3, 224, FC), F32), V((R3, 224, FC), F32), V((R3, 2, 32, D), F32),
            V((UB, D), BF16), V((2, UB, D), BF16), V((UB, D), F32), V((UB, D), F32),
            S.DMA((NT, 8)), S.DMA((WS, 2, 4, 2)), S.DMA((4, 12)), S.DMA((2,)),
            S.DMA((2, 4)), S.DMA((R1, 4)), S.DMA((2, 4)), S.DMA((R2, 4)), S.DMA((2, 3)), S.DMA((R3, 3)),
            S.DMA((2, 6)), S.DMA((3,)), S.DMA((3,)), S.DMA((2 + T // UB,)), S.DMA((7,)),
            S.REGULAR((2,)), S.REGULAR((2,)), S.REGULAR,
        ],
        compiler_params=pltpu.CompilerParams(
            collective_id=0, has_side_effects=True, vmem_limit_bytes=67043328
        ),
    )(h, gout, wgu, wd)[:4]


def solution(mesh):
    tok = P(("dp", "fsdp"))
    stack = P(None, ("dp", "fsdp"))
    wsp = P(None, "fsdp")
    inv = tuple(ORDER.index(k) for k in range(8))

    def local(h, gout, wg, wu, wd):
        def pack(w):
            w = w.reshape(L, 112, 8, NJ, 32)
            w = jnp.stack([w[:, :, k] for k in ORDER], axis=3)
            return jnp.moveaxis(w, 1, 2).reshape(L, NJ, 112, FC)

        def unpack(g):
            g = g.reshape(L, NJ, 112, 8, 32)
            g = jnp.stack([g[:, :, :, k] for k in inv], axis=2)
            return jnp.transpose(g, (0, 3, 2, 1, 4)).reshape(L, 112, FF)

        wgu = jnp.concatenate([pack(wg), pack(wu)], axis=-1)
        og, ou, od, dh = call(h.reshape(L, T, D), gout.reshape(T, D), wgu, wd.reshape(L, NJ, 32, D))
        return unpack(og), unpack(ou), od.reshape(L, 608, D), dh.reshape(1, T, D)

    return jax.shard_map(
        local, mesh=mesh, in_specs=(stack, tok, wsp, wsp, wsp), out_specs=(wsp, wsp, wsp, tok), check_vma=False
    )
```

time: 2010 us -> 1210 us (0.60)
  waiting for transfers between devices: 1130 us -> 0 us
  Pallas kernels: 0 us -> 1090 us
  matrix products: 759 us -> 0 us
  local copies, waits for them, and re-layouts: 50.1 us -> 109 us
  other arithmetic: 50.2 us -> 5.35 us
    pallas_call x0 -> x1, Pallas kernels: none -> 1090 us  [call(): pl.pallas_call(kernel, out_shape=(sd((L, NJ, 112, FC), F32), sd((L, NJ, 1...]
    dot_general x24 -> x0, matrix products: 759 us -> none  [the longest x3 171 us: layer_backward(): jnp.einsum('td,fd->tf', g_bf, down_w, preferred_element_type=jnp.float32)]
    reduce_scatter x9 -> x0, waiting for transfers between devices: 672 us -> none  [reduce_grad(): lax.psum_scatter(local_grad, 'fsdp', scatter_dimension=0, tiled=True)]
    psum x1 -> x0, waiting for transfers between devices: 374 us -> none  [reduce_grad(): return lax.psum(shard_sum, 'dp')]
    all_gather x9 -> x0, waiting for transfers between devices: 77.1 us -> none  [the longest x3 28.3 us: local_backward(): gate_w = lax.all_gather(gate_sh[layer_idx], 'fsdp', axis=0, tiled=True)]
    unnamed x35 -> x42, local copies, waits for them, and re-layouts: 32.9 us -> 70.3 us
  transfers between devices with their start and end apart: 19 -> 0, of which waited for: 10 -> 0; matrix products, arithmetic and copies ran while one was open for 42% -> 0% of each run, Pallas kernels for 0% -> 0%
where the time goes in v1:
time: 1210 us
  Pallas kernels  1090 us (90%)
  local copies, waits for them, and re-layouts  109 us (9%)
    pallas_call x1, Pallas kernels, call(): pl.pallas_call(kernel, out_shape=(sd((L, NJ, 112, FC), F32), sd((L, NJ, 1...  1090 us
    unnamed x42, local copies, waits for them, and re-layouts  70.3 us

profile of v1, /device:TPU:0, one launch (start us, length us, event | category | flops | bytes accessed | tf_op | source)
XLA Modules:
  0.0 1207.8 jit_solution(10091328589095192693)
XLA Ops:
  0.6 5.8 copy.41
  6.5 1.1 fusion.31
  7.5 1.1 fusion.30
  8.6 1.1 fusion.29
  9.7 1.1 fusion.28
  10.8 1.1 fusion.27
  11.9 1.1 fusion.26
  13.0 1.1 fusion.25
  14.1 1.1 fusion.24
  15.2 0.0 copy-start.2
  15.2 1.8 copy-done.2
  17.1 4.5 copy.43
  21.6 5.8 copy.42
  27.5 1.9 fusion.23
  29.4 1.9 fusion.22
  31.2 1.9 fusion.21
  33.1 1.9 fusion.20
  35.0 1.9 fusion.19
  36.9 1.9 fusion.18
  38.7 1.9 fusion.17
  40.6 1.9 fusion.16
  42.5 5.8 copy.44
  48.3 5.4 pad_maximum_fusion.wgu
  53.7 1093.0 %shard_map.84 = (f32[3,19,112,256]{3,2,1,0:T(8,128)}, f32[3,19,112,256]{3,2,1,0:T(8,128)}, f32[3,19,32,896]{3,2,1,0:T(8,128)}, bf16[2048,896]{1,0:T(8,128)(2,1)}...) custom-call(bf16[3,2048,896]{2,1,0:T(8,128)(2,1)} %bitcast.209, ...), custom_call_target="tpu_custom_call" | custom-call | tf_op jit(solution)/shard_map/pallas_call | solution.py:567
  1146.7 8.2 copy.45
  1154.9 0.0 copy-start
  1154.9 1.4 fusion.15
  1156.3 1.5 fusion.14
  1157.8 1.3 fusion.13
  1159.1 1.3 fusion.12
  1160.4 0.0 copy-done
  1160.4 0.1 fusion.11
  1160.5 0.1 fusion.10
  1160.5 0.1 fusion.9
  1160.6 0.1 fusion.8
  1160.7 4.2 copy.53
  1164.9 8.3 copy.63
  1173.2 8.2 copy.54
  1181.4 0.0 copy-start.1
  1181.4 1.4 fusion.7
  1182.8 1.5 fusion.6
  1184.3 1.3 fusion.5
  1185.6 1.3 fusion.4
  1186.9 0.0 copy-done.1
  1186.9 0.1 fusion.3
  1186.9 0.1 fusion.2
  1187.0 0.1 fusion.1
  1187.1 0.1 fusion
  1187.2 4.2 copy.62
  1191.4 8.3 copy.64
  1199.7 0.0 copy-start.3
  1199.7 6.2 copy.109
  1205.9 0.0 copy-done.3
  1205.9 1.8 copy.110
Async XLA Ops:
  15.2 1.9 copy-start.2
  1154.9 5.4 copy-start
  1181.4 5.4 copy-start.1
  1199.7 6.2 copy-start.3

commit v2 on v1

v2 whole, which is shorter than its diff:
```python
import jax
import jax.numpy as jnp
from jax import lax
from jax.experimental import pallas as pl
from jax.experimental.pallas import tpu as pltpu
from jax.sharding import PartitionSpec as P

EPS = 1e-5
MESH = pl.DeviceIdType.MESH
F32, BF16 = jnp.float32, jnp.bfloat16
L, T, D, FF = 3, 2048, 896, 4864
NJ, FC = 19, 256
NI = 10
NT = L * NI
TB, UNROLL = 512, 2
UB = 128
K2, K3, K4 = 3, 6, 8
PF = 10
ND = 2
WS = 16
RS = 16
ORDER = (0, 4, 2, 6, 1, 3, 5, 7)


def dg(a, b, ca, cb):
    return lax.dot_general(a, b, (((ca,), (cb,)), ((), ())), preferred_element_type=F32)


def kernel(h, gout, wgu, wd, og, ou, od, dh0, wbg, wbd, dnx, gbuf,
           hgg, hgu, hgd, h1g, h1u, h1d, p2g, p2u, p2d, h2g, h2u, h2d, p3g, p3u, p3d, h3g, h3u, h3d,
           n_v, gb_v, dn_v, wg_v, wd_v, Gg, Gu, Gd, vg, vu, vd, st_h, st_n, st_dnx, st_g,
           w_recv, w_send, rl_send, load_sem, g_sem, v_sem, p_sem,
           s1_send, s1_recv, s2_send, s2_recv, s3_send, s3_recv,
           o_send, o_recv, x_send, x_recv, st_sem, g_st):
    z, f = lax.axis_index("dp"), lax.axis_index("fsdp")
    y, x, c = f // 4, (f // 2) % 2, f % 2

    def dev(zz, yy, xx, cc):
        return (zz, 4 * yy + 2 * xx + cc)

    xn, yn, zn = dev(z, y, 1 - x, c), dev(z, 1 - y, x, c), dev(1 - z, y, x, c)
    sib = dev(z, y, x, 1 - c)

    def rcopy(src, dst, ss, rs, to):
        return pltpu.make_async_remote_copy(src, dst, ss, rs, device_id=to, device_id_type=MESH)

    def wait_bytes(ref, sem):
        pltpu.make_async_copy(ref, ref, sem).wait()

    bar = pltpu.get_barrier_semaphore()
    for k in range(1, 16):
        g = (8 * z + f + k) % 16
        pl.semaphore_signal(bar, inc=1, device_id=(g // 8, g % 8), device_id_type=MESH)
    pl.semaphore_wait(bar, 15)

    def layer_of(t):
        return L - 1 - t // NI

    def drow(yy, xx, cc):
        return pl.multiple_of(jnp.where(cc == 0, 32 * (2 * xx + yy), 128 + 32 * (2 * yy + xx)), 32)

    def grow(yy, xx, n=224):
        return pl.ds(pl.multiple_of(224 * (2 * yy + xx), 16), n)

    def has(t, cc):
        return 2 * (t % NI) + cc < NJ

    def w_sends(t, cc):
        l, i = layer_of(t), t % NI
        j = 2 * i + cc
        sg, sd = wgu.at[l, j], wd.at[l, j]
        dgu = wbg.at[l, i, pl.ds(pl.multiple_of(112 * f, 16), 112)]
        dd = wbd.at[l, i, pl.ds(drow(y, x, c), 32)]
        direct = t < ND
        prim = jnp.logical_or(direct, t % 2 == z)
        slot = t % WS
        out = []
        for k, (to, cond) in enumerate((
            (dev(z, y, x, cc), cc != c),
            (dev(z, y, 1 - x, cc), prim),
            (dev(z, 1 - y, x, cc), prim),
            (dev(z, 1 - y, 1 - x, cc), direct),
        )):
            out.append((cond, [
                rcopy(sg, dgu, w_send.at[slot, cc, k, 0], w_recv.at[t, 2 * k], to),
                rcopy(sd, dd, w_send.at[slot, cc, k, 1], w_recv.at[t, 2 * k + 1], to),
            ]))
        return out

    def each_send(t, act):
        for cc in range(2):
            @pl.when(has(t, cc))
            def _():
                for cond, cps in w_sends(t, cc):
                    @pl.when(cond)
                    def _():
                        for cp in cps:
                            act(cp)

    def w_issue(t):
        each_send(t, lambda cp: cp.start())

    def w_drain(t):
        each_send(t, lambda cp: cp.wait_send())

    def relay(t, yy, xx, k, to, base):
        l, i = layer_of(t), t % NI
        g = wbg.at[l, i, grow(yy, xx)]
        cps = [rcopy(g, g, rl_send.at[t % RS, base], w_recv.at[t, 2 * k], to)]
        for cc in range(2):
            d = wbd.at[l, i, pl.ds(drow(yy, xx, cc), 32)]
            cps.append(rcopy(d, d, rl_send.at[t % RS, base + 1 + cc], w_recv.at[t, 2 * k + 1], to))
        return cps

    def relays1(t):
        return relay(t, y, 1 - x, 1, zn, 0) + relay(t, 1 - y, x, 2, zn, 3)

    def relays2(t):
        return relay(t, 1 - y, 1 - x, 3, zn, 9)

    def wait_kind(t, k):
        l, i = layer_of(t), t % NI
        wait_bytes(wbg.at[l, i, pl.ds(0, 224)], w_recv.at[t, 2 * k])
        wait_bytes(wbd.at[l, i, pl.ds(0, 64)], w_recv.at[t, 2 * k + 1])

    def relayed(t):
        return jnp.logical_and(t >= ND, jnp.logical_and(t < NT, has(t, c)))

    def w_relay1(t):
        @pl.when(jnp.logical_and(relayed(t), t % 2 == z))
        def _():
            wait_kind(t, 1)
            wait_kind(t, 2)
            for cp in relays1(t):
                cp.start()
            @pl.when((t // 2) % 2 == 0)
            def _():
                for cp in relay(t, y, 1 - x, 3, yn, 6):
                    cp.start()
            @pl.when((t // 2) % 2 == 1)
            def _():
                for cp in relay(t, 1 - y, x, 3, xn, 6):
                    cp.start()

    def w_relay2(t):
        @pl.when(jnp.logical_and(relayed(t), t % 2 == z))
        def _():
            wait_kind(t, 3)
            for cp in relays2(t):
                cp.start()

    def w_relay_drain(t):
        @pl.when(jnp.logical_and(relayed(t), t % 2 == z))
        def _():
            for cp in relays1(t) + relay(t, y, 1 - x, 3, yn, 6) + relays2(t):
                cp.wait_send()

    def loads(t):
        l, i = layer_of(t), t % NI
        s = t % 2
        j = 2 * i + c
        cps = []
        for q in range(4):
            qq = (q + 2 * y + x) % 4
            yy, xx = qq // 2, qq % 2
            if q == 0:
                for mine in (True, False):
                    ff = f if mine else 4 * y + 2 * x + 1 - c
                    cc = c if mine else 1 - c
                    rg, rd = pl.ds(pl.multiple_of(112 * ff, 16), 112), pl.ds(drow(y, x, cc), 32)
                    cps.append((wgu.at[l, j] if mine else wbg.at[l, i, rg], wg_v.at[s, rg]))
                    cps.append((wd.at[l, j] if mine else wbd.at[l, i, rd], wd_v.at[s, rd]))
            else:
                rg = grow(yy, xx)
                cps.append((wbg.at[l, i, rg], wg_v.at[s, rg]))
                for cc in range(2):
                    rd = pl.ds(drow(yy, xx, cc), 32)
                    cps.append((wbd.at[l, i, rd], wd_v.at[s, rd]))
        return cps

    def w_load(t):
        @pl.when(jnp.logical_and(t < NT, has(t, c)))
        def _():
            l, i = layer_of(t), t % NI
            wait_bytes(wbg.at[l, i, pl.ds(0, 112)], w_recv.at[t, 0])
            wait_bytes(wbd.at[l, i, pl.ds(0, 32)], w_recv.at[t, 1])
            @pl.when(jnp.logical_or(t < ND, t % 2 != z))
            def _():
                for k in (1, 2, 3):
                    wait_kind(t, k)
            for src, dst in loads(t):
                pltpu.make_async_copy(src, dst, load_sem.at[0 if src.shape[-1] == 512 else 1]).start()

    def w_load_wait(t):
        wait_bytes(wg_v.at[t % 2], load_sem.at[0])
        wait_bytes(wd_v.at[t % 2], load_sem.at[1])

    for t in range(PF):
        w_issue(jnp.int32(t))

    own0 = T * c
    oth0 = T * (1 - c)

    def rows(base, b):
        return pl.ds(pl.multiple_of(base + b * UB, UB), UB)

    def norm_block(xf):
        r = lax.rsqrt(jnp.mean(xf * xf, axis=-1, keepdims=True) + EPS)
        return r, xf * r

    gl = pltpu.make_async_copy(gout, gb_v.at[pl.ds(pl.multiple_of(own0, T), T)], g_st.at[0])
    gr = rcopy(gout, gb_v.at[pl.ds(pl.multiple_of(own0, T), T)], x_send.at[0], x_recv.at[0], sib)
    gl.start()
    gr.start()

    NB = T // UB

    def h_copy(b):
        return pltpu.make_async_copy(h.at[L - 1, pl.ds(pl.multiple_of(b * UB, UB), UB)], st_n.at[b % 2], st_sem.at[2, b % 2])

    h_copy(jnp.int32(0)).start()

    def first_blocks(b, _):
        @pl.when(b + 1 < NB)
        def _():
            h_copy(b + 1).start()
        h_copy(b).wait()
        _, nf = norm_block(st_n[b % 2].astype(F32))
        ro = rows(own0, b)
        n_v[ro, :] = nf.astype(BF16)
        rcopy(n_v.at[ro], n_v.at[ro], x_send.at[1], x_recv.at[1], sib).start()
        return 0

    lax.fori_loop(0, NB, first_blocks, 0)

    def half(base):
        return pl.ds(pl.multiple_of(base, T), T)

    def exchange_done():
        wait_bytes(n_v.at[half(oth0)], x_recv.at[1])
        wait_bytes(gb_v.at[half(oth0)], x_recv.at[0])
        wait_bytes(n_v.at[half(own0)], x_send.at[1])
        wait_bytes(gb_v.at[half(own0)], x_send.at[0])

    gl.wait()
    w_load(jnp.int32(0))
    exchange_done()

    def compute(s):
        i = s % NI
        ws = s % 2
        w_load_wait(s)
        wg, wdd = wg_v.at[ws], wd_v.at[ws]

        def block(b, _):
            def load(k):
                rw = pl.ds(pl.multiple_of((b * UNROLL + k) * TB, TB), TB)
                return rw, n_v[rw, :], gb_v[rw, :]

            def first(k):
                _, nb, gbb = load(k)
                return dg(nb, wg[...], 1, 0), dg(gbb, wdd[...], 1, 1)

            def middle(uv, da):
                u, v = uv[:, :FC], uv[:, FC:]
                sg = jax.nn.sigmoid(u)
                sl = u * sg
                a = (sl * v).astype(BF16)
                du = (da * v * sg * (1.0 + u * (1.0 - sg))).astype(BF16)
                dv = (da * sl).astype(BF16)
                return a, jnp.concatenate([du, dv], axis=1)

            def second(k, a, duv):
                rw, nb, gbb = load(k)
                dnb = dg(duv, wg[...], 1, 1)
                dn_v[rw, :] = jnp.where(i == 0, 0.0, dn_v[rw, :]) + dnb
                g2 = dg(nb, duv, 0, 0)
                g3 = dg(a, gbb, 0, 0).reshape(8, 32, D)

                def old(ref):
                    return jnp.where(b == 0, 0.0, ref[...]) if k == 0 else ref[...]

                for q in range(4):
                    yy, xx = q // 2, q % 2
                    rg, ru = Gg.at[2 * xx + yy], Gu.at[q]
                    rg[...] = old(rg) + g2[224 * q:224 * q + 224, :FC]
                    ru[...] = old(ru) + g2[224 * q:224 * q + 224, FC:]
                Gd[...] = old(Gd) + g3

            mids = [middle(*first(k)) for k in range(UNROLL)]
            for k in range(UNROLL):
                second(k, *mids[k])
            return 0

        lax.fori_loop(0, 2 * T // (TB * UNROLL), block, 0)

    def valid(s):
        return jnp.logical_and(jnp.logical_and(s >= 0, s < NT), 2 * (s % NI) + c < NJ)

    def when_valid(s):
        return pl.when(valid(s))

    def s1(s):
        ax, ay = pl.ds(2 * (1 - x), 2), pl.ds(2 * (1 - y), 2)
        by = pl.ds(4 + 2 * (1 - y), 2)
        return [
            rcopy(hgg.at[s, ax], h1g.at[s], s1_send.at[s, 0], s1_recv.at[s, 0], xn),
            rcopy(hgd.at[s, ax], h1d.at[s, pl.ds(0, 2)], s1_send.at[s, 1], s1_recv.at[s, 1], xn),
            rcopy(hgu.at[s, ay], h1u.at[s], s1_send.at[s, 2], s1_recv.at[s, 2], yn),
            rcopy(hgd.at[s, by], h1d.at[s, pl.ds(2, 2)], s1_send.at[s, 3], s1_recv.at[s, 3], yn),
        ]

    def s2(s):
        return [
            rcopy(p2g.at[s], h2g.at[s], s2_send.at[s, 0], s2_recv.at[s, 0], yn),
            rcopy(p2d.at[s, 0], h2d.at[s, 0], s2_send.at[s, 1], s2_recv.at[s, 1], yn),
            rcopy(p2u.at[s], h2u.at[s], s2_send.at[s, 2], s2_recv.at[s, 2], xn),
            rcopy(p2d.at[s, 1], h2d.at[s, 1], s2_send.at[s, 3], s2_recv.at[s, 3], xn),
        ]

    def s3(s):
        return [
            rcopy(p3g.at[s], h3g.at[s], s3_send.at[s, 0], s3_recv.at[s, 0], zn),
            rcopy(p3u.at[s], h3u.at[s], s3_send.at[s, 1], s3_recv.at[s, 1], zn),
            rcopy(p3d.at[s], h3d.at[s], s3_send.at[s, 2], s3_recv.at[s, 2], zn),
        ]

    def outs(s):
        l, j = layer_of(s), 2 * (s % NI) + c
        mine, other = pl.ds(pl.multiple_of(112 * c, 8), 112), pl.ds(pl.multiple_of(112 * (1 - c), 8), 112)
        local = [
            pltpu.make_async_copy(vg.at[5, mine], og.at[l, j], o_send.at[0]),
            pltpu.make_async_copy(vu.at[5, mine], ou.at[l, j], o_send.at[1]),
            pltpu.make_async_copy(vd.at[5, c], od.at[l, j], o_send.at[2]),
        ]
        remote = [
            rcopy(vg.at[5, other], og.at[l, j], o_send.at[3], o_recv.at[0], sib),
            rcopy(vu.at[5, other], ou.at[l, j], o_send.at[4], o_recv.at[1], sib),
            rcopy(vd.at[5, 1 - c], od.at[l, j], o_send.at[5], o_recv.at[2], sib),
        ]
        return local + remote

    def fetch(slot, g, u, d0, d1):
        pltpu.make_async_copy(g, vg.at[slot], v_sem.at[slot, 0]).start()
        pltpu.make_async_copy(u, vu.at[slot], v_sem.at[slot, 1]).start()
        pltpu.make_async_copy(d0, vd.at[slot, 0], v_sem.at[slot, 2]).start()
        pltpu.make_async_copy(d1, vd.at[slot, 1], v_sem.at[slot, 3]).start()

    def fetched(*slots):
        for k in slots:
            wait_bytes(vg.at[k], v_sem.at[k, 0])
            wait_bytes(vu.at[k], v_sem.at[k, 1])
            wait_bytes(vd.at[k, 0], v_sem.at[k, 2])
            wait_bytes(vd.at[k, 1], v_sem.at[k, 3])

    def add(slot, *more):
        for r in (vg, vu, vd):
            t = r[slot]
            for k in more:
                t = t + r[k]
            r[slot] = t

    def arrive(cps):
        for cp in cps:
            cp.wait_recv()

    def begin(s):
        m2, m3, m4 = s - K2, s - K3, s - K4

        @when_valid(m4 - 1)
        def _():
            cps = outs(m4 - 1)
            for cp in cps[:3]:
                cp.wait()
            for cp in cps[3:]:
                cp.wait_send()

        @when_valid(m2)
        def _():
            arrive(s1(m2))
            fetch(0, hgg.at[m2, 2 * x + 1 - y], hgu.at[m2, 2 * y + 1 - x], hgd.at[m2, 2 * x + 1 - y], hgd.at[m2, 4 + 2 * y + 1 - x])
            fetch(1, h1g.at[m2, 1 - y], h1u.at[m2, 1 - x], h1d.at[m2, 1 - y], h1d.at[m2, 3 - x])

        @when_valid(m3)
        def _():
            arrive(s2(m3))
            fetch(2, hgg.at[m3, 2 * x + y], hgu.at[m3, 2 * y + x], hgd.at[m3, 2 * x + y], hgd.at[m3, 4 + 2 * y + x])
            fetch(3, h1g.at[m3, y], h1u.at[m3, x], h1d.at[m3, y], h1d.at[m3, 2 + x])
            fetch(4, h2g.at[m3], h2u.at[m3], h2d.at[m3, 0], h2d.at[m3, 1])

        @when_valid(m4)
        def _():
            arrive(s3(m4))
            fetch(5, p3g.at[m4], p3u.at[m4], p3d.at[m4, 0], p3d.at[m4, 1])
            fetch(6, h3g.at[m4], h3u.at[m4], h3d.at[m4, 0], h3d.at[m4, 1])

    def put(slot, k, g, u, d):
        return [
            pltpu.make_async_copy(vg.at[slot], g, p_sem.at[k, 0]),
            pltpu.make_async_copy(vu.at[slot], u, p_sem.at[k, 1]),
            pltpu.make_async_copy(vd.at[slot], d, p_sem.at[k, 2]),
        ]

    def start(cps):
        for cp in cps:
            cp.start()

    def finish(s):
        m2, m3, m4 = s - K2, s - K3, s - K4

        def store_g():
            return [
                pltpu.make_async_copy(Gg, hgg.at[s], g_sem.at[0]),
                pltpu.make_async_copy(Gu, hgu.at[s], g_sem.at[1]),
                pltpu.make_async_copy(Gd, hgd.at[s], g_sem.at[2]),
            ]

        @when_valid(s)
        def _():
            start(store_g())

        @when_valid(m3)
        def _():
            fetched(2, 3, 4)
            add(2, 3, 4)
            start(put(2, 1, p3g.at[m3], p3u.at[m3], p3d.at[m3]))

        @when_valid(m2)
        def _():
            fetched(0, 1)
            add(0, 1)
            start(put(0, 0, p2g.at[m2], p2u.at[m2], p2d.at[m2]))

        @when_valid(m4)
        def _():
            fetched(5, 6)
            add(5, 6)
            start(outs(m4))

        @when_valid(m3)
        def _():
            for cp in put(2, 1, p3g.at[m3], p3u.at[m3], p3d.at[m3]):
                cp.wait()
            start(s3(m3))

        @when_valid(m2)
        def _():
            for cp in put(0, 0, p2g.at[m2], p2u.at[m2], p2d.at[m2]):
                cp.wait()
            start(s2(m2))

        @when_valid(s)
        def _():
            for cp in store_g():
                cp.wait()
            start(s1(s))

    DX = 4

    def dn_send():
        for b in range(DX):
            w = T // DX
            src = dn_v.at[pl.ds(pl.multiple_of(oth0 + b * w, w), w)]
            rcopy(src, dnx.at[pl.ds(b * w, w)], x_send.at[2], x_recv.at[2 + b], sib).start()

    def boundary(s):
        l = layer_of(s)

        def copies(b):
            r = pl.ds(pl.multiple_of(b * UB, UB), UB)
            k = b % 2
            return (
                pltpu.make_async_copy(h.at[l, r], st_h.at[k], st_sem.at[0, k]),
                pltpu.make_async_copy(dnx.at[r], st_dnx.at[k], st_sem.at[1, k]),
                pltpu.make_async_copy(h.at[jnp.maximum(l - 1, 0), r], st_n.at[k], st_sem.at[2, k]),
                pltpu.make_async_copy(gbuf.at[r], st_g.at[k], st_sem.at[3, k]),
            )

        def each(b, act):
            ch, cd, cn, cg = copies(b)
            act(ch)
            act(cd)

            @pl.when(l > 0)
            def _():
                act(cn)

            @pl.when(l < L - 1)
            def _():
                act(cg)

        def fetch_block(b):
            @pl.when(b % (NB // DX) == 0)
            def _():
                wait_bytes(dnx.at[pl.ds(0, T // DX)], x_recv.at[2 + b // (NB // DX)])
            each(b, lambda cp: cp.start())

        def g_out(b):
            k = b % 2
            return pltpu.make_async_copy(st_g.at[k], gbuf.at[pl.ds(pl.multiple_of(b * UB, UB), UB)], g_st.at[k])

        fetch_block(jnp.int32(0))

        def block(b, _):
            k = b % 2
            r = pl.ds(pl.multiple_of(b * UB, UB), UB)
            ro = rows(own0, b)

            @pl.when(jnp.logical_and(l > 0, b > 0))
            def _():
                g_out(b - 1).wait()

            @pl.when(b + 1 < NB)
            def _():
                fetch_block(b + 1)

            each(b, lambda cp: cp.wait())

            @pl.when(l == L - 1)
            def _():
                st_g[k] = gb_v[ro, :].astype(F32)

            rr, nf = norm_block(st_h[k].astype(F32))
            dn = dn_v[ro, :] + st_dnx[k]
            m = jnp.mean(dn * nf, axis=-1, keepdims=True)
            g = st_g[k] + rr * (dn - nf * m)
            gb_v[ro, :] = g.astype(BF16)

            @pl.when(l > 0)
            def _():
                st_g[k] = g
                g_out(b).start()
                _, nf2 = norm_block(st_n[k].astype(F32))
                n_v[ro, :] = nf2.astype(BF16)
                rcopy(gb_v.at[ro], gb_v.at[ro], x_send.at[0], x_recv.at[0], sib).start()
                rcopy(n_v.at[ro], n_v.at[ro], x_send.at[1], x_recv.at[1], sib).start()

            @pl.when(l == 0)
            def _():
                pltpu.make_async_copy(gb_v.at[ro], dh0.at[r], g_st.at[2]).start()
            return 0

        lax.fori_loop(0, NB, block, 0)
        wait_bytes(dn_v.at[half(oth0)], x_send.at[2])

        @pl.when(l > 0)
        def _():
            g_out(jnp.int32(NB - 1)).wait()
            exchange_done()

        @pl.when(l == 0)
        def _():
            wait_bytes(dh0, g_st.at[2])

    def step(s, _):
        edge = jnp.logical_and(s % NI == NI - 1, s < NT)

        @pl.when(s < 5)
        def _():
            w_relay1(2 * s + 2)
            w_relay1(2 * s + 3)

        @pl.when(s >= 5)
        def _():
            w_relay1(s + 7)

        @pl.when(jnp.logical_and(s >= 1, s < 4))
        def _():
            w_relay2(2 * s)
            w_relay2(2 * s + 1)

        @pl.when(s >= 4)
        def _():
            w_relay2(s + 4)

        begin(s)

        @when_valid(s)
        def _():
            compute(s)

        @pl.when(edge)
        def _():
            dn_send()

        finish(s)

        @pl.when(s + PF < NT)
        def _():
            @pl.when(s + PF >= WS)
            def _():
                w_drain(s + PF - WS)
            w_issue(s + PF)

        w_load(s + 1)

        @pl.when(edge)
        def _():
            boundary(s)

        w_relay_drain(s - 2)
        return 0

    lax.fori_loop(0, NT + K4 + 2, step, 0)

    def settle(s, _):
        @when_valid(s)
        def _():
            for cp in s1(s) + s2(s) + s3(s):
                cp.wait_send()
        return 0

    lax.fori_loop(0, NT, settle, 0)
    for t in range(NT - WS, NT):
        w_drain(jnp.int32(t))

    def out_done(cnt):
        wait_bytes(og.at[:, pl.ds(0, cnt)], o_recv.at[0])
        wait_bytes(ou.at[:, pl.ds(0, cnt)], o_recv.at[1])
        wait_bytes(od.at[:, pl.ds(0, cnt)], o_recv.at[2])

    @pl.when(c == 0)
    def _():
        out_done(9)

    @pl.when(c == 1)
    def _():
        out_done(10)


def call(h, gout, wgu, wd):
    A = pl.BlockSpec(memory_space=pl.ANY)
    V, S = pltpu.VMEM, pltpu.SemaphoreType
    sd = jax.ShapeDtypeStruct
    return pl.pallas_call(
        kernel,
        out_shape=(
            sd((L, NJ, 112, FC), F32), sd((L, NJ, 112, FC), F32), sd((L, NJ, 32, D), F32), sd((T, D), BF16),
            sd((L, NI, D, 2 * FC), BF16), sd((L, NI, FC, D), BF16), sd((T, D), F32), sd((T, D), F32),
            sd((NT, 4, 224, FC), F32), sd((NT, 4, 224, FC), F32), sd((NT, 8, 32, D), F32),
            sd((NT, 2, 224, FC), F32), sd((NT, 2, 224, FC), F32), sd((NT, 4, 32, D), F32),
        ) + (sd((NT, 224, FC), F32), sd((NT, 224, FC), F32), sd((NT, 2, 32, D), F32)) * 4,
        in_specs=[A] * 4,
        out_specs=(A,) * 26,
        scratch_shapes=[
            V((2 * T, D), BF16), V((2 * T, D), BF16), V((2 * T, D), F32),
            V((2, D, 2 * FC), BF16), V((2, FC, D), BF16),
            V((4, 224, FC), F32), V((4, 224, FC), F32), V((8, 32, D), F32),
            V((7, 224, FC), F32), V((7, 224, FC), F32), V((7, 2, 32, D), F32),
            V((2, UB, D), BF16), V((2, UB, D), BF16), V((2, UB, D), F32), V((2, UB, D), F32),
            S.DMA((NT, 8)), S.DMA((WS, 2, 4, 2)), S.DMA((RS, 12)), S.DMA((2,)), S.DMA((3,)), S.DMA((7, 4)), S.DMA((2, 3)),
            S.DMA((NT, 4)), S.DMA((NT, 4)), S.DMA((NT, 4)), S.DMA((NT, 4)), S.DMA((NT, 3)), S.DMA((NT, 3)),
            S.DMA((6,)), S.DMA((3,)), S.DMA((3,)), S.DMA((6,)), S.DMA((4, 2)), S.DMA((3,)),
        ],
        compiler_params=pltpu.CompilerParams(
            collective_id=0, has_side_effects=True, vmem_limit_bytes=67043328
        ),
    )(h, gout, wgu, wd)[:4]


def pack_kernel(wg, wu, out):
    for m, w in enumerate((wg, wu)):
        for j in range(NJ):
            cols = [w[0, :, 608 * d + 32 * j:608 * d + 32 * j + 32] for d in ORDER]
            out[0, j, :, FC * m:FC * m + FC] = jnp.concatenate(cols, axis=1)


def pack(wg, wu):
    return pl.pallas_call(
        pack_kernel,
        grid=(L,),
        out_shape=jax.ShapeDtypeStruct((L, NJ, 112, 2 * FC), BF16),
        in_specs=[pl.BlockSpec((1, 112, FF), lambda l: (l, 0, 0))] * 2,
        out_specs=pl.BlockSpec((1, NJ, 112, 2 * FC), lambda l: (l, 0, 0, 0)),
    )(wg, wu)


def unpack_kernel(a, b, out_a, out_b):
    for g, o in ((a, out_a), (b, out_b)):
        for t in range(FF // 128):
            parts = []
            for col in range(128 * t, 128 * t + 128, 32):
                p, j = ORDER.index(col // 608), (col % 608) // 32
                parts.append(g[0, j, :, 32 * p:32 * p + 32])
            o[0, :, 128 * t:128 * t + 128] = jnp.concatenate(parts, axis=1)


def unpack(a, b):
    rb = 56
    return pl.pallas_call(
        unpack_kernel,
        grid=(L, 112 // rb),
        out_shape=(jax.ShapeDtypeStruct((L, 112, FF), F32),) * 2,
        in_specs=[pl.BlockSpec((1, NJ, rb, FC), lambda l, r: (l, 0, r, 0))] * 2,
        out_specs=(pl.BlockSpec((1, rb, FF), lambda l, r: (l, r, 0)),) * 2,
    )(a, b)


def solution(mesh):
    tok = P(("dp", "fsdp"))
    stack = P(None, ("dp", "fsdp"))
    wsp = P(None, "fsdp")

    def local(h, gout, wg, wu, wd):
        og, ou, od, dh = call(h.reshape(L, T, D), gout.reshape(T, D), pack(wg, wu), wd.reshape(L, NJ, 32, D))
        og, ou = unpack(og, ou)
        return og, ou, od.reshape(L, 608, D), dh.reshape(1, T, D)

    return jax.shard_map(
        local, mesh=mesh, in_specs=(stack, tok, wsp, wsp, wsp), out_specs=(wsp, wsp, wsp, tok), check_vma=False
    )
```

time: 1210 us -> 937 us (0.77)
  Pallas kernels: 1090 us -> 926 us
  local copies, waits for them, and re-layouts: 109 us -> 8.05 us
    pallas_call x1, Pallas kernels: 1090 us -> 904 us  [call(): pl.pallas_call(kernel, out_shape=(sd((L, NJ, 112, FC), F32), sd((L, NJ, 1...]
    unnamed x42 -> x4, local copies, waits for them, and re-layouts: 70.3 us -> 8.05 us
    pallas_call x0 -> x2, Pallas kernels: none -> 22.8 us  [the longest x1 14.1 us: unpack(): pl.pallas_call(unpack_kernel, grid=(L, 112 // rb), out_shape=(jax.ShapeDt...]
    pallas_call x2 -> x0, local copies, waits for them, and re-layouts: 16.4 us -> none  [call(): pl.pallas_call(kernel, out_shape=(sd((L, NJ, 112, FC), F32), sd((L, NJ, 1...]
where the time goes in v2:
time: 937 us; the launch traced here: 935 us
  Pallas kernels  926 us (99%)
    pallas_call x1, Pallas kernels, call(): pl.pallas_call(kernel, out_shape=(sd((L, NJ, 112, FC), F32), sd((L, NJ, 1...  904 us

profile of v2, /device:TPU:0, one launch (start us, length us, event | category | flops | bytes accessed | tf_op | source)
XLA Modules:
  0.0 935.1 jit_solution(1474311578580005270)
XLA Ops:
  0.6 8.8 shard_map.84.wgu
  9.4 903.6 %shard_map.85 = (f32[3,19,112,256]{3,2,1,0:T(8,128)}, f32[3,19,112,256]{3,2,1,0:T(8,128)}, f32[3,19,32,896]{3,2,1,0:T(8,128)}, bf16[2048,896]{1,0:T(8,128)(2,1)}...) custom-call(bf16[3,2048,896]{2,1,0:T(8,128)(2,1)} %bitcast.5, ...), custom_call_target="tpu_custom_call" | custom-call | tf_op jit(solution)/shard_map/pallas_call | solution.py:635
  913.0 14.1 %shard_map.86 = (f32[3,112,4864]{2,1,0:T(8,128)}, f32[3,112,4864]{2,1,0:T(8,128)}) custom-call(f32[3,19,112,256]{3,2,1,0:T(8,128)} %get-tuple-element.10.a, f32[3,19,112,256]{3,2,1,0:T(8,128)} %get-tuple-element.11.b), custom_call_target="tpu_custom_call" | custom-call | tf_op jit(solution)/shard_map/pallas_call | solution.py:690
  927.0 0.0 copy-start
  927.0 6.2 copy.11
  933.3 0.0 copy-done
  933.3 1.8 copy.12
Async XLA Ops:
  927.0 6.2 copy-start

commit v3 on v0

v3 whole, which is shorter than its diff:
```python
import jax
import jax.numpy as jnp
from jax import lax
from jax.experimental import pallas as pl
from jax.experimental.pallas import tpu as pltpu
from jax.sharding import PartitionSpec as P

EPS = 1e-5
MESH = pl.DeviceIdType.MESH
F32, BF16 = jnp.float32, jnp.bfloat16
L, T, D, FF = 3, 2048, 896, 4864
RW, RD = 112, 608
CW, DW = 224, 32
NJ, FC = 19, 256
FC2 = 2 * FC
NI = 10
NT = L * NI
TB, UNROLL = 512, 2
UB = 128
NB = T // UB
DX = 4
K2, K3, K4 = 3, 5, 7
PF = 8
RING = 12
SD = 4
ND = 16
ORDER = (0, 4, 2, 6, 1, 3, 5, 7)
OWN, VX, VY, DIAG = range(4)
both = jnp.logical_and


def dg(a, b, ca, cb):
    return lax.dot_general(a, b, (((ca,), (cb,)), ((), ())), preferred_element_type=F32)


def rcopy(src, dst, ss, rs, to):
    return pltpu.make_async_remote_copy(src, dst, ss, rs, device_id=to, device_id_type=MESH)


def lcopy(src, dst, sem):
    return pltpu.make_async_copy(src, dst, sem)


def wait_bytes(ref, sem):
    lcopy(ref, ref, sem).wait()


def start(cps):
    for cp in cps:
        cp.start()


def arrive(cps):
    for cp in cps:
        cp.wait_recv()


def leave(cps):
    for cp in cps:
        cp.wait_send()


def span(base, n, align):
    return pl.ds(pl.multiple_of(base, align), n)


def norm_block(xb):
    xf = xb.astype(F32)
    r = lax.rsqrt(jnp.mean(xf * xf, axis=-1, keepdims=True) + EPS)
    return r, xf * r


def kernel(h, gout, wgu, wd, og, ou, od, dh0, wbg, wbd, dnx, gbuf,
           hg, hd, h1g, h1d, p2g, p2d, h2g, h2d, p3g, p3d, h3g, h3d,
           n_v, gb_v, dn_v, wg_v, wd_v, Gg, Gd, vg, vd, st_h, st_n, st_dnx, st_g,
           w_recv, w_send, rl_send, load_sem, g_sem, v_sem, p_sem,
           s1_send, s1_recv, s2_send, s2_recv, s3_send, s3_recv,
           o_send, o_recv, gb_x, n_x, dn_send_sem, dn_recv_sem, st_sem, g_st, dh_sem):
    z, f = lax.axis_index("dp"), lax.axis_index("fsdp")
    y, x, c = f // 4, (f // 2) % 2, f % 2
    X, Y, C = 1 - x, 1 - y, 1 - c

    def dev(zz, yy, xx, cc):
        return (zz, 4 * yy + 2 * xx + cc)

    xn, yn, zn, sib = dev(z, y, X, c), dev(z, Y, x, c), dev(1 - z, y, x, c), dev(z, y, x, C)

    bar = pltpu.get_barrier_semaphore()
    for k in range(1, ND):
        o = (8 * z + f + k) % ND
        pl.semaphore_signal(bar, inc=1, device_id=(o // 8, o % 8), device_id_type=MESH)
    pl.semaphore_wait(bar, ND - 1)

    def where_of(t):
        return L - 1 - t // NI, t % NI

    def drow(yy, xx, cc):
        return span(DW * jnp.where(cc == 0, 2 * xx + yy, 4 + 2 * yy + xx), DW, DW)

    def grow(yy, xx):
        return span(CW * (2 * yy + xx), CW, 16)

    def has(t, cc):
        return both(both(t >= 0, t < NT), 2 * (t % NI) + cc < NJ)

    def primary(t):
        return t % 2 == z

    def w_sends(t, cc):
        l, i = where_of(t)
        j = 2 * i + cc
        ends = ((wgu.at[l, j], wbg.at[l, i, span(RW * f, RW, 16)]), (wd.at[l, j], wbd.at[l, i, drow(y, x, c)]))
        targets = ((dev(z, y, x, cc), cc != c), (dev(z, y, X, cc), primary(t)), (dev(z, Y, x, cc), primary(t)))
        return [
            (cond, [
                rcopy(src, dst, w_send.at[t % RING, cc, k, m], w_recv.at[t, k, m], to)
                for m, (src, dst) in enumerate(ends)
            ])
            for k, (to, cond) in enumerate(targets)
        ]

    def each_send(t, act):
        for cc in range(2):
            @pl.when(has(t, cc))
            def _():
                for cond, cps in w_sends(t, cc):
                    @pl.when(cond)
                    def _():
                        act(cps)

    def relay_to(t, yy, xx, kind, to, base):
        l, i = where_of(t)
        cuts = [(wbg, grow(yy, xx), 0)] + [(wbd, drow(yy, xx, cc), 1) for cc in range(2)]
        return [
            rcopy(b.at[l, i, r], b.at[l, i, r], rl_send.at[t % RING, base, k], w_recv.at[t, kind, m], to)
            for k, (b, r, m) in enumerate(cuts)
        ]

    def x_to_z(t):
        return relay_to(t, y, X, VX, zn, VX)

    def y_to_z(t):
        return relay_to(t, Y, x, VY, zn, VY)

    def x_to_y(t):
        return relay_to(t, y, X, DIAG, yn, OWN)

    def y_to_x(t):
        return relay_to(t, Y, x, DIAG, xn, OWN)

    def diag_to_z(t):
        return relay_to(t, Y, X, DIAG, zn, DIAG)

    def wait_kind(t, k):
        l, i = where_of(t)
        wait_bytes(wbg.at[l, i, pl.ds(0, CW)], w_recv.at[t, k, 0])
        wait_bytes(wbd.at[l, i, pl.ds(0, 2 * DW)], w_recv.at[t, k, 1])

    def when_relay(t):
        return pl.when(both(has(t, c), primary(t)))

    def w_relay1(t):
        @when_relay(t)
        def _():
            wait_kind(t, VX)
            wait_kind(t, VY)
            start(x_to_z(t) + y_to_z(t))
            by_y = (t // 2) % 2 == 0

            @pl.when(by_y)
            def _():
                start(x_to_y(t))

            @pl.when(jnp.logical_not(by_y))
            def _():
                start(y_to_x(t))

    def w_relay2(t):
        @when_relay(t)
        def _():
            wait_kind(t, DIAG)
            start(diag_to_z(t))

    def w_relay_drain(t):
        @when_relay(t)
        def _():
            leave(x_to_z(t) + y_to_z(t) + x_to_y(t) + diag_to_z(t))

    def w_load(t):
        @pl.when(has(t, c))
        def _():
            l, i = where_of(t)
            s, j = t % 2, 2 * i + c
            wait_bytes(wbg.at[l, i, pl.ds(0, RW)], w_recv.at[t, OWN, 0])
            wait_bytes(wbd.at[l, i, pl.ds(0, DW)], w_recv.at[t, OWN, 1])

            @pl.when(jnp.logical_not(primary(t)))
            def _():
                for k in (VX, VY, DIAG):
                    wait_kind(t, k)

            mine = span(RW * f, RW, 16), drow(y, x, c)
            theirs = span(RW * (f + C - c), RW, 16), drow(y, x, C)
            gs = [(wgu.at[l, j], mine[0]), (wbg.at[l, i, theirs[0]], theirs[0])]
            ds = [(wd.at[l, j], mine[1]), (wbd.at[l, i, theirs[1]], theirs[1])]
            for yy, xx in ((y, X), (Y, x), (Y, X)):
                gs.append((wbg.at[l, i, grow(yy, xx)], grow(yy, xx)))
                for cc in range(2):
                    ds.append((wbd.at[l, i, drow(yy, xx, cc)], drow(yy, xx, cc)))
            for m, (v, cuts) in enumerate(((wg_v, gs), (wd_v, ds))):
                for src, r in cuts:
                    lcopy(src, v.at[s, r], load_sem.at[m]).start()

    def w_start(lo, hi):
        for t in range(lo, hi):
            each_send(jnp.int32(t), start)

    w_start(0, 2)

    own0, oth0 = T * c, T * C
    mine, theirs = span(own0, T, T), span(oth0, T, T)

    def rows(b):
        return span(own0 + b * UB, UB, UB)

    def block_rows(b):
        return span(b * UB, UB, UB)

    def pass_rows(v, ro, sems):
        rcopy(v.at[ro], v.at[ro], sems.at[0], sems.at[1], sib).start()

    gl = lcopy(gout, gb_v.at[mine], dh_sem)
    gl.start()
    rcopy(gout, gb_v.at[mine], gb_x.at[0], gb_x.at[1], sib).start()

    def h_copy(b):
        return lcopy(h.at[L - 1, block_rows(b)], st_n.at[b % SD], st_sem.at[0, b % SD])

    for b in range(SD - 1):
        h_copy(jnp.int32(b)).start()

    def first_blocks(b, _):
        @pl.when(b + SD - 1 < NB)
        def _():
            h_copy(b + SD - 1).start()

        h_copy(b).wait()
        n_v[rows(b), :] = norm_block(st_n[b % SD])[1].astype(BF16)
        pass_rows(n_v, rows(b), n_x)
        return 0

    lax.fori_loop(0, NB, first_blocks, 0)

    def exchange_done():
        for v, sems in ((n_v, n_x), (gb_v, gb_x)):
            wait_bytes(v.at[mine], sems.at[0])
            wait_bytes(v.at[theirs], sems.at[1])

    gl.wait()
    for act, lo, hi in ((w_relay1, 2, 4), (w_relay2, 4, PF)):
        for t in range(2):
            act(jnp.int32(t))
        w_start(lo, hi)
    w_load(jnp.int32(0))
    exchange_done()

    def compute(s, hooks):
        i, ws = s % NI, s % 2
        wait_bytes(wg_v.at[ws], load_sem.at[0])
        wait_bytes(wd_v.at[ws], load_sem.at[1])
        wg, wdd = wg_v.at[ws], wd_v.at[ws]

        def block(b, _):
            for k, hook in enumerate(hooks):
                pl.when(b == k + 1)(hook)

            def load(k):
                rw = span((b * UNROLL + k) * TB, TB, TB)
                return rw, n_v[rw, :], gb_v[rw, :]

            def first(k):
                _, nb, gbb = load(k)
                return dg(nb, wg[...], 1, 0), dg(gbb, wdd[...], 1, 1)

            def middle(uv, da):
                u, v = uv[:, :FC], uv[:, FC:]
                sg = jax.nn.sigmoid(u)
                sl = u * sg
                a = (sl * v).astype(BF16)
                du = (da * v * sg * (1.0 + u * (1.0 - sg))).astype(BF16)
                dv = (da * sl).astype(BF16)
                return a, jnp.concatenate([du, dv], axis=1)

            def second(k, a, duv):
                rw, nb, gbb = load(k)
                dn_v[rw, :] = jnp.where(i == 0, 0.0, dn_v[rw, :]) + dg(duv, wg[...], 1, 1)
                g2 = dg(nb, duv, 0, 0)
                g3 = dg(a, gbb, 0, 0).reshape(Gd.shape[1:])

                def old(ref):
                    return jnp.where(b == 0, 0.0, ref[...]) if k == 0 else ref[...]

                for q in range(4):
                    part = g2[CW * q:CW * q + CW]
                    rg, ru = Gg.at[ws, 0, 2 * (q % 2) + q // 2], Gg.at[ws, 1, q]
                    rg[...] = old(rg) + part[:, :FC]
                    ru[...] = old(ru) + part[:, FC:]
                rd = Gd.at[ws]
                rd[...] = old(rd) + g3

            mids = [middle(*first(k)) for k in range(UNROLL)]
            for k in range(UNROLL):
                second(k, *mids[k])
            return 0

        lax.fori_loop(0, 2 * T // (TB * UNROLL), block, 0)

    COLORS = ((x, y, xn, yn), (y, x, yn, xn))

    def valid(s):
        return has(s, c)

    def when_valid(s):
        return pl.when(valid(s))

    def s1(s):
        return [
            rcopy(src.at[s, k, pl.ds(2 * (1 - a), 2)], dst.at[s, k], s1_send.at[s, k, m], s1_recv.at[s, k, m], to)
            for k, (a, _, to, _) in enumerate(COLORS)
            for m, (src, dst) in enumerate(((hg, h1g), (hd, h1d)))
        ]

    def s2(s):
        return [
            rcopy(src.at[s, k], dst.at[s, k], s2_send.at[s, k, m], s2_recv.at[s, k, m], to)
            for k, (_, _, _, to) in enumerate(COLORS)
            for m, (src, dst) in enumerate(((p2g, h2g), (p2d, h2d)))
        ]

    def s3(s):
        return [
            rcopy(src.at[s], dst.at[s], s3_send.at[s, m], s3_recv.at[s, m], zn)
            for m, (src, dst) in enumerate(((p3g, h3g), (p3d, h3d)))
        ]

    A0, A1, B0, B1, B2, C0, C1 = range(7)

    def outs(s):
        l, i = where_of(s)
        j = 2 * i + c
        cps = []
        for m, (cc, to) in enumerate(((c, None), (C, sib))):
            half = span(RW * cc, RW, 16)
            ends = ((vg.at[C0, 0, half], og), (vg.at[C0, 1, half], ou), (vd.at[C0, cc], od))
            for k, (src, dst) in enumerate(ends):
                sem = o_send.at[m, k]
                cps.append(rcopy(src, dst.at[l, j], sem, o_recv.at[k], to) if m else lcopy(src, dst.at[l, j], sem))
        return cps

    def fetch(slot, pick):
        for k, (a, b, _, _) in enumerate(COLORS):
            for m, (v, src) in enumerate(zip((vg, vd), pick(k, a, b))):
                lcopy(src, v.at[slot, k], v_sem.at[slot, k, m]).start()

    def add(slot, *more):
        for q in (slot, *more):
            for k in range(2):
                wait_bytes(vg.at[q, k], v_sem.at[q, k, 0])
                wait_bytes(vd.at[q, k], v_sem.at[q, k, 1])
        for r in (vg, vd):
            t = r[slot]
            for q in more:
                t = t + r[q]
            r[slot] = t

    def at(g, d, *ix):
        return g.at[ix], d.at[ix]

    def begin(tick):
        m2, m3, m4 = tick - K2, tick - K3, tick - K4

        @when_valid(m4 - 1)
        def _():
            cps = outs(m4 - 1)
            for cp in cps[:L]:
                cp.wait()
            leave(cps[L:])

        @when_valid(m4)
        def _():
            arrive(s3(m4))
            fetch(C0, lambda k, a, b: at(p3g, p3d, m4, k))
            fetch(C1, lambda k, a, b: at(h3g, h3d, m4, k))

        @when_valid(m3)
        def _():
            arrive(s2(m3))
            fetch(B0, lambda k, a, b: at(hg, hd, m3, k, 2 * a + b))
            fetch(B1, lambda k, a, b: at(h1g, h1d, m3, k, b))
            fetch(B2, lambda k, a, b: at(h2g, h2d, m3, k))

        @when_valid(m2)
        def _():
            arrive(s1(m2))
            fetch(A0, lambda k, a, b: at(hg, hd, m2, k, 2 * a + 1 - b))
            fetch(A1, lambda k, a, b: at(h1g, h1d, m2, k, 1 - b))

    def put(slot, g, d):
        return [lcopy(v.at[slot], dst, p_sem.at[slot, m]) for m, (v, dst) in enumerate(((vg, g), (vd, d)))]

    def keep(s):
        return [lcopy(v.at[s % 2], dst.at[s], g_sem.at[m]) for m, (v, dst) in enumerate(((Gg, hg), (Gd, hd)))]

    def put2(s):
        return put(A0, p2g.at[s], p2d.at[s])

    def put3(s):
        return put(B0, p3g.at[s], p3d.at[s])

    def wait_all(cps):
        for cp in cps:
            cp.wait()

    def sums(tick):
        m2, m3, m4 = tick - K2, tick - K3, tick - K4

        @when_valid(m3)
        def _():
            add(B0, B1, B2)
            start(put3(m3))

        @when_valid(m2)
        def _():
            add(A0, A1)
            start(put2(m2))

        @when_valid(m4)
        def _():
            add(C0, C1)
            start(outs(m4))

    def send_sums(tick):
        m2, m3 = tick - K2, tick - K3

        @when_valid(m3)
        def _():
            wait_all(put3(m3))
            start(s3(m3))

        @when_valid(m2)
        def _():
            wait_all(put2(m2))
            start(s2(m2))

    def send_first(s):
        @when_valid(s)
        def _():
            wait_all(keep(s))
            start(s1(s))

    def dn_send():
        w = T // DX
        for b in range(DX):
            src = dn_v.at[span(oth0 + b * w, w, w)]
            rcopy(src, dnx.at[pl.ds(b * w, w)], dn_send_sem, dn_recv_sem.at[b], sib).start()

    def boundary(s):
        l, _ = where_of(s)

        def each(b, act):
            r, k = block_rows(b), b % SD
            lower = jnp.maximum(l - 1, 0)
            cps = [
                lcopy(src, dst.at[k], st_sem.at[m, k])
                for m, (src, dst) in enumerate(((h.at[lower, r], st_n), (h.at[l, r], st_h), (dnx.at[r], st_dnx), (gbuf.at[r], st_g)))
            ]
            act(cps[1])
            act(cps[2])

            @pl.when(l > 0)
            def _():
                act(cps[0])

            @pl.when(l < L - 1)
            def _():
                act(cps[3])

        def fetch_block(b):
            per = NB // DX

            @pl.when(b % per == 0)
            def _():
                wait_bytes(dnx.at[pl.ds(0, T // DX)], dn_recv_sem.at[b // per])

            each(b, lambda cp: cp.start())

        def g_out(b):
            return lcopy(st_g.at[b % SD], gbuf.at[block_rows(b)], g_st.at[b % SD])

        for b in range(SD - 1):
            fetch_block(jnp.int32(b))

        def block(b, _):
            k, ro = b % SD, rows(b)

            @pl.when(both(l > 0, b > 0))
            def _():
                g_out(b - 1).wait()

            @pl.when(b + SD - 1 < NB)
            def _():
                fetch_block(b + SD - 1)

            each(b, lambda cp: cp.wait())

            @pl.when(l == L - 1)
            def _():
                st_g[k] = gb_v[ro, :].astype(F32)

            rr, nf = norm_block(st_h[k])
            dn = dn_v[ro, :] + st_dnx[k]
            g = st_g[k] + rr * (dn - nf * jnp.mean(dn * nf, axis=-1, keepdims=True))
            gb_v[ro, :] = g.astype(BF16)

            @pl.when(l > 0)
            def _():
                st_g[k] = g
                g_out(b).start()
                n_v[ro, :] = norm_block(st_n[k])[1].astype(BF16)
                pass_rows(gb_v, ro, gb_x)
                pass_rows(n_v, ro, n_x)

            @pl.when(l == 0)
            def _():
                lcopy(gb_v.at[ro], dh0.at[block_rows(b)], dh_sem).start()

            return 0

        lax.fori_loop(0, NB, block, 0)
        wait_bytes(dn_v.at[theirs], dn_send_sem)

        @pl.when(l > 0)
        def _():
            g_out(NB - 1).wait()
            exchange_done()

        @pl.when(l == 0)
        def _():
            wait_bytes(dh0, dh_sem)

    def is_edge(s):
        return both(s % NI == NI - 1, both(s >= 0, s < NT))

    def step(s, _):
        edge = is_edge(s)
        busy = valid(s)

        @pl.when(s < 3)
        def _():
            w_relay1(2 * s + 2)
            w_relay1(2 * s + 3)

        @pl.when(s >= 3)
        def _():
            w_relay1(s + PF - 3)

        @pl.when(both(s >= 1, s < 3))
        def _():
            w_relay2(2 * s)
            w_relay2(2 * s + 1)

        @pl.when(s >= 3)
        def _():
            w_relay2(s + 3)

        def arrivals():
            @pl.when(jnp.logical_not(is_edge(s - 1)))
            def _():
                send_first(s - 1)

            begin(s)

        def departures():
            send_sums(s)
            w_load(s + 1)

        parts = (arrivals, lambda: sums(s), departures)

        @pl.when(jnp.logical_not(busy))
        def _():
            for part in parts:
                part()

        @pl.when(busy)
        def _():
            compute(s, parts)
            start(keep(s))

        each_send(s + PF - RING, leave)
        each_send(s + PF, start)

        @pl.when(edge)
        def _():
            dn_send()
            send_first(s)
            boundary(s)

        w_relay_drain(s - 2)
        return 0

    lax.fori_loop(0, NT + K4 + 1, step, 0)

    def settle(s, _):
        @when_valid(s)
        def _():
            leave(s1(s) + s2(s) + s3(s))

        return 0

    lax.fori_loop(0, NT, settle, 0)

    def out_done(cnt):
        for k, o in enumerate((og, ou, od)):
            wait_bytes(o.at[:, pl.ds(0, cnt)], o_recv.at[k])

    for cc in range(2):
        @pl.when(c == cc)
        def _():
            out_done(NI - 1 + cc)


def call(h, gout, wgu, wd):
    A = pl.BlockSpec(memory_space=pl.ANY)
    V, S = pltpu.VMEM, pltpu.SemaphoreType
    sd = jax.ShapeDtypeStruct

    def pair(*lead):
        return (*lead, CW, FC), (*lead, DW, D)

    grads = [sd(s, F32) for lead in ((NT, 2, 4), (NT, 2, 2)) + ((NT, 2),) * 4 for s in pair(*lead)]
    return pl.pallas_call(
        kernel,
        out_shape=(
            sd((L, NJ, RW, FC), F32), sd((L, NJ, RW, FC), F32), sd((L, NJ, DW, D), F32), sd((T, D), BF16),
            sd((L, NI, D, FC2), BF16), sd((L, NI, FC, D), BF16), sd((T, D), F32), sd((T, D), F32), *grads,
        ),
        in_specs=[A] * 4,
        out_specs=(A,) * (8 + len(grads)),
        scratch_shapes=[
            V((2 * T, D), BF16), V((2 * T, D), BF16), V((2 * T, D), F32),
            V((2, D, FC2), BF16), V((2, FC, D), BF16),
            *(V(s, F32) for s in pair(2, 2, 4)), *(V(s, F32) for s in pair(7, 2)),
            *(V((SD, UB, D), t) for t in (BF16, BF16, F32, F32)),
            S.DMA((NT, 4, 2)), S.DMA((RING, 2, 3, 2)), S.DMA((RING, 4, 3)), S.DMA((2,)), S.DMA((2,)), S.DMA((7, 2, 2)), S.DMA((7, 2)),
            *(S.DMA((NT, 2, 2)) for _ in range(4)), *(S.DMA((NT, 2)) for _ in range(2)),
            S.DMA((2, 3)), S.DMA((3,)), S.DMA((2,)), S.DMA((2,)), S.DMA, S.DMA((DX,)), S.DMA((4, SD)), S.DMA((SD,)), S.DMA,
        ],
        compiler_params=pltpu.CompilerParams(
            collective_id=0, has_side_effects=True, vmem_limit_bytes=67043328
        ),
    )(h, gout, wgu, wd)[:4]


def pack_kernel(wg, wu, out):
    for m, w in enumerate((wg, wu)):
        for j in range(NJ):
            cols = [w[0, :, RD * d + DW * j:RD * d + DW * j + DW] for d in ORDER]
            out[0, j, :, FC * m:FC * m + FC] = jnp.concatenate(cols, axis=1)


def pack(wg, wu):
    return pl.pallas_call(
        pack_kernel,
        grid=(L,),
        out_shape=jax.ShapeDtypeStruct((L, NJ, RW, FC2), BF16),
        in_specs=[pl.BlockSpec((1, RW, FF), lambda l: (l, 0, 0))] * 2,
        out_specs=pl.BlockSpec((1, NJ, RW, FC2), lambda l: (l, 0, 0, 0)),
    )(wg, wu)


def unpack_kernel(a, b, d, e, out_a, out_b, out_d, out_e):
    for g, o in ((a, out_a), (b, out_b)):
        for t in range(FF // UB):
            parts = []
            for col in range(UB * t, UB * t + UB, DW):
                p, j = ORDER.index(col // RD), (col % RD) // DW
                parts.append(g[0, j, :, DW * p:DW * p + DW])
            o[0, :, UB * t:UB * t + UB] = jnp.concatenate(parts, axis=1)
    out_d[...] = d[...]
    out_e[...] = e[...]


def unpack(a, b, d, e):
    rb, db, eb = RW // 2, RD // 2, T // 4
    sd = jax.ShapeDtypeStruct
    dspec = pl.BlockSpec((1, db, D), lambda l, r: (l, r, 0))
    espec = pl.BlockSpec((eb, D), lambda l, r: (jnp.minimum(2 * l + r, 3), 0))
    return pl.pallas_call(
        unpack_kernel,
        grid=(L, 2),
        out_shape=(sd((L, RW, FF), F32), sd((L, RW, FF), F32), sd(d.shape, F32), sd(e.shape, BF16)),
        in_specs=[pl.BlockSpec((1, NJ, rb, FC), lambda l, r: (l, 0, r, 0))] * 2 + [dspec, espec],
        out_specs=(pl.BlockSpec((1, rb, FF), lambda l, r: (l, r, 0)),) * 2 + (dspec, espec),
    )(a, b, d, e)


def solution(mesh):
    tok = P(("dp", "fsdp"))
    stack = P(None, ("dp", "fsdp"))
    wsp = P(None, "fsdp")

    def local(h, gout, wg, wu, wd):
        og, ou, od, dh = call(h.reshape(L, T, D), gout.reshape(T, D), pack(wg, wu), wd.reshape(L, NJ, DW, D))
        og, ou, od, dh = unpack(og, ou, od.reshape(L, RD, D), dh)
        return og, ou, od, dh.reshape(1, T, D)

    return jax.shard_map(
        local, mesh=mesh, in_specs=(stack, tok, wsp, wsp, wsp), out_specs=(wsp, wsp, wsp, tok), check_vma=False
    )
```

time: 2010 us -> 889 us (0.44)
  waiting for transfers between devices: 1130 us -> 0 us
  Pallas kernels: 0 us -> 885 us
  matrix products: 759 us -> 0 us
  other arithmetic: 50.2 us -> 0 us
  local copies, waits for them, and re-layouts: 50.1 us -> 0 us
    pallas_call x0 -> x3, Pallas kernels: none -> 885 us  [the longest x1 855 us: call(): pl.pallas_call(kernel, out_shape=(sd((L, NJ, RW, FC), F32), sd((L, NJ, RW...]
    dot_general x24 -> x0, matrix products: 759 us -> none  [the longest x3 171 us: layer_backward(): jnp.einsum('td,fd->tf', g_bf, down_w, preferred_element_type=jnp.float32)]
    reduce_scatter x9 -> x0, waiting for transfers between devices: 672 us -> none  [reduce_grad(): lax.psum_scatter(local_grad, 'fsdp', scatter_dimension=0, tiled=True)]
    psum x1 -> x0, waiting for transfers between devices: 374 us -> none  [reduce_grad(): return lax.psum(shard_sum, 'dp')]
    all_gather x9 -> x0, waiting for transfers between devices: 77.1 us -> none  [the longest x3 28.3 us: local_backward(): gate_w = lax.all_gather(gate_sh[layer_idx], 'fsdp', axis=0, tiled=True)]
    unnamed x35 -> x0, local copies, waits for them, and re-layouts: 32.9 us -> none
  transfers between devices with their start and end apart: 19 -> 0, of which waited for: 10 -> 0; matrix products, arithmetic and copies ran while one was open for 42% -> 0% of each run, Pallas kernels for 0% -> 0%
where the time goes in v3:
time: 889 us; the launch traced here: 885 us
  Pallas kernels  885 us (100%)
    pallas_call x1, Pallas kernels, call(): pl.pallas_call(kernel, out_shape=(sd((L, NJ, RW, FC), F32), sd((L, NJ, RW...  855 us
    pallas_call x1, Pallas kernels, unpack(): pl.pallas_call(unpack_kernel, grid=(L, 2), out_shape=(sd((L, RW, FF), F32...  20.6 us

profile of v3, /device:TPU:0, one launch (start us, length us, event | category | flops | bytes accessed | tf_op | source)
XLA Modules:
  0.0 885.3 jit_solution(13152783699757597115)
XLA Ops:
  0.6 8.8 shard_map.84.wgu
  9.4 855.3 %shard_map.85 = (f32[3,19,112,256]{3,2,1,0:T(8,128)}, f32[3,19,112,256]{3,2,1,0:T(8,128)}, f32[3,19,32,896]{3,2,1,0:T(8,128)}, bf16[2048,896]{1,0:T(8,128)(2,1)}...) custom-call(bf16[3,2048,896]{2,1,0:T(8,128)(2,1)} %bitcast.5, ...), custom_call_target="tpu_custom_call" | custom-call | tf_op jit(solution)/shard_map/pallas_call | solution.py:641
  864.7 20.6 %shard_map.86 = (f32[3,112,4864]{2,1,0:T(8,128)}, f32[3,112,4864]{2,1,0:T(8,128)}, f32[3,608,896]{2,1,0:T(8,128)}, bf16[2048,896]{1,0:T(8,128)(2,1)}) custom-call(f32[3,19,112,256]{3,2,1,0:T(8,128)} %get-tuple-element.12.a, f32[3,19,112,256]{3,2,1,0:T(8,128)} %get-tuple-element.13.b, f32[3,608,896]{2,1,0:T(8,128)} %bitcast.6, ...), custom_call_target="tpu_custom_call" | custom-call | tf_op jit(solution)/shard_map/pallas_call | solution.py:698

commit v4 on v3

--- a/solution.py
+++ b/solution.py
@@ -15,6 +15,7 @@
 FC2 = 2 * FC
 NI = 10
 NT = L * NI
+LAST = NT - 1
 TB, UNROLL = 512, 2
 UB = 128
 NB = T // UB
@@ -376,8 +377,11 @@
     def at(g, d, *ix):
         return g.at[ix], d.at[ix]
 
+    def second(s):
+        return jnp.where(s < LAST + K2, s - K2, jnp.where(s == LAST + K3 - 1, LAST, -1))
+
     def begin(tick):
-        m2, m3, m4 = tick - K2, tick - K3, tick - K4
+        m2, m3, m4 = second(tick), tick - K3, tick - K4
 
         @when_valid(m4 - 1)
         def _():
@@ -422,7 +426,7 @@
             cp.wait()
 
     def sums(tick):
-        m2, m3, m4 = tick - K2, tick - K3, tick - K4
+        m2, m3, m4 = second(tick), tick - K3, tick - K4
 
         @when_valid(m3)
         def _():
@@ -440,7 +444,7 @@
             start(outs(m4))
 
     def send_sums(tick):
-        m2, m3 = tick - K2, tick - K3
+        m2, m3 = second(tick), tick - K3
 
         @when_valid(m3)
         def _():
@@ -602,8 +606,16 @@
         @pl.when(edge)
         def _():
             dn_send()
-            send_first(s)
-            boundary(s)
+
+        inner = both(edge, s < LAST)
+
+        @pl.when(jnp.logical_or(inner, s == LAST + K2 - 1))
+        def _():
+            send_first(jnp.where(inner, s, LAST))
+
+        @pl.when(jnp.logical_or(inner, s == LAST + K3))
+        def _():
+            boundary(jnp.where(inner, s, LAST))
 
         w_relay_drain(s - 2)
         return 0

time: 889 us -> 880 us (0.990)
  no operation moved by 1% of the time
where the time goes in v4:
time: 880 us
  Pallas kernels  879 us (100%)
    pallas_call x1, Pallas kernels, call(): pl.pallas_call(kernel, out_shape=(sd((L, NJ, RW, FC), F32), sd((L, NJ, RW...  850 us
    pallas_call x1, Pallas kernels, unpack(): pl.pallas_call(unpack_kernel, grid=(L, 2), out_shape=(sd((L, RW, FF), F32...  20.6 us

profile of v4, /device:TPU:0, one launch (start us, length us, event | category | flops | bytes accessed | tf_op | source)
XLA Modules:
  0.0 879.6 jit_solution(17866306592959346866)
XLA Ops:
  0.6 8.8 shard_map.84.wgu
  9.4 849.5 %shard_map.85 = (f32[3,19,112,256]{3,2,1,0:T(8,128)}, f32[3,19,112,256]{3,2,1,0:T(8,128)}, f32[3,19,32,896]{3,2,1,0:T(8,128)}, bf16[2048,896]{1,0:T(8,128)(2,1)}...) custom-call(bf16[3,2048,896]{2,1,0:T(8,128)(2,1)} %bitcast.5, ...), custom_call_target="tpu_custom_call" | custom-call | tf_op jit(solution)/shard_map/pallas_call | solution.py:653
  858.9 20.6 %shard_map.86 = (f32[3,112,4864]{2,1,0:T(8,128)}, f32[3,112,4864]{2,1,0:T(8,128)}, f32[3,608,896]{2,1,0:T(8,128)}, bf16[2048,896]{1,0:T(8,128)(2,1)}) custom-call(f32[3,19,112,256]{3,2,1,0:T(8,128)} %get-tuple-element.12.a, f32[3,19,112,256]{3,2,1,0:T(8,128)} %get-tuple-element.13.b, f32[3,608,896]{2,1,0:T(8,128)} %bitcast.6, ...), custom_call_target="tpu_custom_call" | custom-call | tf_op jit(solution)/shard_map/pallas_call | solution.py:710

commit v5 on v4

--- a/solution.py
+++ b/solution.py
@@ -51,6 +51,11 @@
         cp.start()
 
 
+def wait_all(cps):
+    for cp in cps:
+        cp.wait()
+
+
 def arrive(cps):
     for cp in cps:
         cp.wait_recv()
@@ -71,9 +76,9 @@
     return r, xf * r
 
 
-def kernel(h, gout, wgu, wd, og, ou, od, dh0, wbg, wbd, dnx, gbuf,
+def kernel(h, gout, w_gate, w_up, wd, og, ou, od, dh0, wgu, wbg, wbd, dnx, gbuf,
            hg, hd, h1g, h1d, p2g, p2d, h2g, h2d, p3g, p3d, h3g, h3d,
-           n_v, gb_v, dn_v, wg_v, wd_v, Gg, Gd, vg, vd, st_h, st_n, st_dnx, st_g,
+           n_v, gb_v, dn_v, raw_v, packed_v, wg_v, wd_v, Gg, Gd, vg, vd, st_h, st_n, st_dnx, st_g,
            w_recv, w_send, rl_send, load_sem, g_sem, v_sem, p_sem,
            s1_send, s1_recv, s2_send, s2_recv, s3_send, s3_recv,
            o_send, o_recv, gb_x, n_x, dn_send_sem, dn_recv_sem, st_sem, g_st, dh_sem):
@@ -212,6 +217,19 @@
                 for src, r in cuts:
                     lcopy(src, v.at[s, r], load_sem.at[m]).start()
 
+    def pack(l):
+        cps = [lcopy(w.at[l], raw_v.at[m], st_sem.at[m, 0]) for m, w in enumerate((w_gate, w_up))]
+        start(cps)
+        wait_all(cps)
+        for j in range(NJ):
+            cols = [raw_v[m, :, RD * d + DW * j:RD * d + DW * j + DW] for m in range(2) for d in ORDER]
+            packed_v[j] = jnp.concatenate(cols, axis=1)
+        cp = lcopy(packed_v, wgu.at[l], st_sem.at[2, 0])
+        cp.start()
+        cp.wait()
+
+    pack(L - 1)
+
     def w_start(lo, hi):
         for t in range(lo, hi):
             each_send(jnp.int32(t), start)
@@ -421,10 +439,6 @@
     def put3(s):
         return put(B0, p3g.at[s], p3d.at[s])
 
-    def wait_all(cps):
-        for cp in cps:
-            cp.wait()
-
     def sums(tick):
         m2, m3, m4 = second(tick), tick - K3, tick - K4
 
@@ -559,6 +573,12 @@
         edge = is_edge(s)
         busy = valid(s)
 
+        pack_at = both(s % 2 == 1, s < 2 * L - 2)
+
+        @pl.when(pack_at)
+        def _():
+            pack(L - 2 - s // 2)
+
         @pl.when(s < 3)
         def _():
             w_relay1(2 * s + 2)
@@ -641,7 +661,7 @@
             out_done(NI - 1 + cc)
 
 
-def call(h, gout, wgu, wd):
+def call(h, gout, wg, wu, wd):
     A = pl.BlockSpec(memory_space=pl.ANY)
     V, S = pltpu.VMEM, pltpu.SemaphoreType
     sd = jax.ShapeDtypeStruct
@@ -654,13 +674,13 @@
         kernel,
         out_shape=(
             sd((L, NJ, RW, FC), F32), sd((L, NJ, RW, FC), F32), sd((L, NJ, DW, D), F32), sd((T, D), BF16),
-            sd((L, NI, D, FC2), BF16), sd((L, NI, FC, D), BF16), sd((T, D), F32), sd((T, D), F32), *grads,
+            sd((L, NJ, RW, FC2), BF16), sd((L, NI, D, FC2), BF16), sd((L, NI, FC, D), BF16), sd((T, D), F32), sd((T, D), F32), *grads,
         ),
-        in_specs=[A] * 4,
-        out_specs=(A,) * (8 + len(grads)),
+        in_specs=[A] * 5,
+        out_specs=(A,) * (9 + len(grads)),
         scratch_shapes=[
             V((2 * T, D), BF16), V((2 * T, D), BF16), V((2 * T, D), F32),
-            V((2, D, FC2), BF16), V((2, FC, D), BF16),
+            V((2, RW, FF), BF16), V((NJ, RW, FC2), BF16), V((2, D, FC2), BF16), V((2, FC, D), BF16),
             *(V(s, F32) for s in pair(2, 2, 4)), *(V(s, F32) for s in pair(7, 2)),
             *(V((SD, UB, D), t) for t in (BF16, BF16, F32, F32)),
             S.DMA((NT, 4, 2)), S.DMA((RING, 2, 3, 2)), S.DMA((RING, 4, 3)), S.DMA((2,)), S.DMA((2,)), S.DMA((7, 2, 2)), S.DMA((7, 2)),
@@ -670,24 +690,7 @@
         compiler_params=pltpu.CompilerParams(
             collective_id=0, has_side_effects=True, vmem_limit_bytes=67043328
         ),
-    )(h, gout, wgu, wd)[:4]
-
-
-def pack_kernel(wg, wu, out):
-    for m, w in enumerate((wg, wu)):
-        for j in range(NJ):
-            cols = [w[0, :, RD * d + DW * j:RD * d + DW * j + DW] for d in ORDER]
-            out[0, j, :, FC * m:FC * m + FC] = jnp.concatenate(cols, axis=1)
-
-
-def pack(wg, wu):
-    return pl.pallas_call(
-        pack_kernel,
-        grid=(L,),
-        out_shape=jax.ShapeDtypeStruct((L, NJ, RW, FC2), BF16),
-        in_specs=[pl.BlockSpec((1, RW, FF), lambda l: (l, 0, 0))] * 2,
-        out_specs=pl.BlockSpec((1, NJ, RW, FC2), lambda l: (l, 0, 0, 0)),
-    )(wg, wu)
+    )(h, gout, wg, wu, wd)[:4]
 
 
 def unpack_kernel(a, b, d, e, out_a, out_b, out_d, out_e):
@@ -722,7 +725,7 @@
     wsp = P(None, "fsdp")
 
     def local(h, gout, wg, wu, wd):
-        og, ou, od, dh = call(h.reshape(L, T, D), gout.reshape(T, D), pack(wg, wu), wd.reshape(L, NJ, DW, D))
+        og, ou, od, dh = call(h.reshape(L, T, D), gout.reshape(T, D), wg, wu, wd.reshape(L, NJ, DW, D))
         og, ou, od, dh = unpack(og, ou, od.reshape(L, RD, D), dh)
         return og, ou, od, dh.reshape(1, T, D)
 

time: 880 us -> 879 us (level)
  no operation moved by 1% of the time
where the time goes in v5:
time: 879 us; the launch traced here: 878 us
  Pallas kernels  877 us (100%)
    pallas_call x1, Pallas kernels, call(): pl.pallas_call(kernel, out_shape=(sd((L, NJ, RW, FC), F32), sd((L, NJ, RW...  857 us
    pallas_call x1, Pallas kernels, unpack(): pl.pallas_call(unpack_kernel, grid=(L, 2), out_shape=(sd((L, RW, FF), F32...  20.6 us

profile of v5, /device:TPU:0, one launch (start us, length us, event | category | flops | bytes accessed | tf_op | source)
XLA Modules:
  0.0 878.1 jit_solution(17804941926022549928)
XLA Ops:
  0.6 856.8 %shard_map.84 = (f32[3,19,112,256]{3,2,1,0:T(8,128)}, f32[3,19,112,256]{3,2,1,0:T(8,128)}, f32[3,19,32,896]{3,2,1,0:T(8,128)}, bf16[2048,896]{1,0:T(8,128)(2,1)}...) custom-call(bf16[3,2048,896]{2,1,0:T(8,128)(2,1)} %bitcast.5, ...), custom_call_target="tpu_custom_call" | custom-call | tf_op jit(solution)/shard_map/pallas_call | solution.py:673
  857.5 20.6 %shard_map.85 = (f32[3,112,4864]{2,1,0:T(8,128)}, f32[3,112,4864]{2,1,0:T(8,128)}, f32[3,608,896]{2,1,0:T(8,128)}, bf16[2048,896]{1,0:T(8,128)(2,1)}) custom-call(f32[3,19,112,256]{3,2,1,0:T(8,128)} %get-tuple-element.12.a, f32[3,19,112,256]{3,2,1,0:T(8,128)} %get-tuple-element.13.b, f32[3,608,896]{2,1,0:T(8,128)} %bitcast.6, ...), custom_call_target="tpu_custom_call" | custom-call | tf_op jit(solution)/shard_map/pallas_call | solution.py:713
